TPU v7x, 32 devices: a whole 2x2x4 slice. The times are simulated.
32 devices in a mesh: rel: 4 (over z), node: 2 (over x), head: 4 (over y, core).
Axes of the slice: x: 2, y: 2, z: 4, core: 2. Of those that a mesh axis runs over, the one named last changes fastest.
Arguments:
- features: bfloat16 [4096, 512], P('node'), may hold values from -26 to 26
- node_type: int32 [4096], P('node'), may hold values from 0 to 3
- w_query: bfloat16 [4, 512, 512], P(None, None, 'head'), may hold values from -0.25 to 0.25
- w_key: bfloat16 [4, 512, 512], P(None, None, 'head'), may hold values from -0.25 to 0.25
- w_value: bfloat16 [4, 512, 512], P(None, None, 'head'), may hold values from -0.25 to 0.25
- rel_att: bfloat16 [64, 8, 64, 64], P(None, 'head'), may hold values from -0.75 to 0.75
- rel_msg: bfloat16 [64, 8, 64, 64], P(None, 'head'), may hold values from -0.75 to 0.75
- rel_prior: float32 [64, 8], P(None, 'head'), may hold values from 0.5 to 3
- w_out: bfloat16 [4, 512, 512], P(None, 'head'), may hold values from -0.25 to 0.25
- skip: float32 [4], replicated, may hold values from -1.5 to 1.5
- rel_perm: int32 [64], P('rel'), may hold values from 0 to 63, each once
- tile_src: int32 [64, 32], P('rel', 'node'), may hold values from 0 to 31
- tile_dst: int32 [64, 32], P('rel', 'node'), may hold values from 0 to 15
- tile_bits: int32 [64, 32, 128, 4], P('rel', 'node'), may hold values from -2147483648 to 2147483646
- tile_count: int32 [64, 2], P('rel', 'node'), may hold values from 1 to 16, as said below
Outputs:
- updated: bfloat16 [4096, 512], P(('node', 'head'))
Inputs may be any that keep to these rules, and one draw needn't show every extreme that they name: The first tile_count[p, g] slots of group g of position p are live; the words of the other slots may have bits set, but those bits give no edges and must be ignored. Some position has all 16 slots live in every group.
All inputs are finite; a program needn't handle non-finite values.
Results may differ from a plain program's by a relative error of at most 0.008.
The roundings to bfloat16 on the way count: a program that leaves them out, or rounds other values in their place, can miss the bound.
Values may be sent and summed in bfloat16 or wider, within the bound.
A program may use at most 128 MiB of HBM per device.

v0:
```python
import functools
import math

import jax
import jax.numpy as jnp
from jax import lax
from jax.experimental import pallas as pl
from jax.experimental.pallas import tpu as pltpu
from jax.sharding import PartitionSpec as P

NEG = -1e30
FLOOR = -1e29
GROUP = 4
CHUNK = 4
PAD_ROWS = 16
VMEM_BYTES = 30 * 1024 * 1024


def column(types_row):
    size = types_row.shape[1]
    return jnp.broadcast_to(types_row.astype(jnp.float32), (size, size)).T


def bits_for(count):
    return max(int(count - 1).bit_length(), 1)


def own_block(local, per, n_rel, r):
    return (local // per) * per * n_rel + r * per + local % per


def project_rows(x, weights):
    return [jnp.dot(x, w, preferred_element_type=jnp.float32) for w in weights]


def compact(meta, own_blocks, per, n_rel, r, fields, list_ref):
    src_bits, dst_bits, slot_bits, rel_bits, own_bits = fields
    rows, lanes = meta.shape
    live = meta >= 0
    src = meta & ((1 << src_bits) - 1)
    dst = lax.shift_right_logical(meta, src_bits) & ((1 << dst_bits) - 1)
    rel = lax.shift_right_logical(meta, src_bits + dst_bits) & ((1 << rel_bits) - 1)
    slot = lax.broadcasted_iota(jnp.int32, meta.shape, 0) * lanes + lax.broadcasted_iota(jnp.int32, meta.shape, 1)
    base = slot | lax.shift_left(src, slot_bits) | lax.shift_left(rel, slot_bits + src_bits)
    top = slot_bits + src_bits + rel_bits
    base = base | (1 << (top + own_bits))
    bf = jnp.bfloat16
    hits = [live & (dst == own_block(d, per, n_rel, r)) for d in range(own_blocks)]
    flags = jnp.concatenate([jnp.where(hit, 1.0, 0.0) for hit in hits], axis=0).astype(bf)
    size = own_blocks * rows
    before = lax.broadcasted_iota(jnp.int32, (lanes, lanes), 0) < lax.broadcasted_iota(jnp.int32, (lanes, lanes), 1)
    in_row = jnp.dot(flags, jnp.where(before, 1.0, 0.0).astype(bf), preferred_element_type=jnp.float32)
    row_sum = jnp.dot(flags, jnp.ones((lanes, lanes), bf), preferred_element_type=jnp.float32).astype(bf)
    i = lax.broadcasted_iota(jnp.int32, (size, size), 0)
    j = lax.broadcasted_iota(jnp.int32, (size, size), 1)
    same = jnp.zeros((size, size), jnp.bool_)
    for d in range(own_blocks):
        lo, hi = d * rows, (d + 1) * rows
        same = same | ((i >= lo) & (i < hi) & (j >= lo) & (j < hi))
    ahead = jnp.where(same & (j < i), 1.0, 0.0).astype(bf)
    both = jnp.where(same, 1.0, 0.0).astype(bf)
    rows_before = jnp.dot(ahead, row_sum, preferred_element_type=jnp.float32)
    totals = jnp.dot(both, row_sum, preferred_element_type=jnp.float32)
    rank = jnp.full(meta.shape, -1.0, jnp.float32)
    entry = base
    start = jnp.zeros(meta.shape, jnp.float32)
    for d in range(own_blocks):
        part = slice(d * rows, (d + 1) * rows)
        place = start + rows_before[part] + in_row[part]
        rank = jnp.where(hits[d], place, rank)
        entry = jnp.where(hits[d], base | (d << top), entry)
        start = start + jnp.floor((totals[part] + (GROUP - 1)) * (1.0 / GROUP)) * GROUP
    pieces = [(lax.shift_right_logical(entry, 8 * q) & 255).astype(jnp.float32) for q in range(4)]
    row_entries = []
    for a in range(rows):
        parts = [piece[a : a + 1] for piece in pieces] + [jnp.zeros((4, lanes), jnp.float32)]
        row_entries.append(jnp.concatenate(parts, axis=0).astype(bf))
    places = lax.broadcasted_iota(jnp.int32, (lanes, lanes), 0).astype(jnp.float32)
    for k in range(list_ref.shape[0] - 1):
        ids = places + float(k * lanes)
        found = jnp.zeros((8, lanes), jnp.float32)
        for a in range(rows):
            hot = jnp.where(ids == rank[a : a + 1], 1.0, 0.0).astype(bf)
            found = found + lax.dot_general(
                row_entries[a], hot, (((1,), (1,)), ((), ())), preferred_element_type=jnp.float32
            )
        whole = found.astype(jnp.int32)
        line = whole[0:1]
        for q in range(1, 4):
            line = line | lax.shift_left(whole[q : q + 1], 8 * q)
        list_ref[k : k + 1] = line
    groups = (start[0:1] * (1.0 / GROUP)).astype(jnp.int32)
    list_ref[list_ref.shape[0] - 1 :] = groups


def prepare_kernel(n_rel, n_node, n_head, fields, *refs):
    (packed_ref, types_ref, feat_ref, wk_ref, wv_ref, wq_ref, att_ref, msg_ref, wout_ref, bits_ref) = refs[:10]
    (k_all, vt_all, qt_ref, att_out, msg_out, bits_all, w_all, list_ref) = refs[10:18]
    (x_v, wk_v, wv_v, wq_v, att_v, msg_v, meta_all) = refs[18:25]
    (local, z_send, z_recv, y_send, y_recv, d_send, d_recv, m_send, m_recv, x_send, x_recv, o_send, o_recv) = refs[25:]
    blocks = types_ref.shape[0]
    block = types_ref.shape[1]
    cols = wk_v.shape[2]
    kinds = wk_v.shape[0]
    slots = bits_ref.shape[0]
    share = slots // n_head
    own_blocks = qt_ref.shape[0]
    per = own_blocks // n_head
    chunks = blocks // CHUNK
    rows = CHUNK * block
    relations, heads, size = att_v.shape[0], att_v.shape[1], att_v.shape[2]
    r = lax.axis_index("rel")
    n = lax.axis_index("node")
    h = lax.axis_index("head")
    sibling = h + 1 - 2 * lax.rem(h, 2)
    pairs = list(range(2, n_head, 2))
    bf = jnp.bfloat16

    def fetch(src, dst, index):
        copy = pltpu.make_async_copy(src, dst, local.at[index])
        copy.start()
        return copy

    own_bits = fetch(bits_ref, bits_all.at[pl.ds(pl.multiple_of(r * slots, slots), slots)], 0)
    got_w = [fetch(wk_ref, wk_v, 1), fetch(wv_ref, wv_v, 2)]
    got_x = []
    for c in range(chunks):
        got_x.append(fetch(feat_ref.at[pl.ds(c * rows, rows)], x_v.at[pl.ds(c * rows, rows)], 8 + c))
    got_q = fetch(wq_ref, wq_v, 3)
    got_rel = [fetch(att_ref, att_v, 4), fetch(msg_ref, msg_v, 5)]
    got_out = fetch(wout_ref, w_all.at[h], 6)

    barrier = pltpu.get_barrier_semaphore()
    for t in range(1, n_rel):
        pl.semaphore_signal(barrier, inc=1, device_id={"rel": lax.rem(r + t, n_rel)})
    for t in range(1, n_node):
        pl.semaphore_signal(barrier, inc=1, device_id={"node": lax.rem(n + t, n_node)})
    for t in pairs:
        pl.semaphore_signal(barrier, inc=1, device_id={"head": lax.rem(h + t, n_head)})
    pl.semaphore_signal(barrier, inc=1, device_id={"head": sibling})
    meta_all[pl.ds(r, 1)] = packed_ref[...].reshape((1,) + packed_ref.shape)
    pl.semaphore_wait(barrier, n_rel - 1 + n_node - 1 + len(pairs) + 1)

    started = []

    def send(src, dst, send_sem, recv_sem, target):
        copy = pltpu.make_async_remote_copy(
            src_ref=src, dst_ref=dst, send_sem=send_sem, recv_sem=recv_sem, device_id=target
        )
        copy.start()
        started.append(copy)
        return copy

    def bit_rows(rel, head):
        return bits_all.at[pl.ds(pl.multiple_of(rel * slots + head * share, share), share)]

    own_bits.wait()
    metas, zs = [], []
    for t in range(1, n_rel):
        target = {"rel": lax.rem(r + t, n_rel)}
        metas.append(send(meta_all.at[r], meta_all.at[r], m_send.at[t], m_recv.at[t], target))
    for t in range(1, n_rel):
        target = {"rel": lax.rem(r + t, n_rel)}
        zs.append(send(bit_rows(r, h), bit_rows(r, h), z_send.at[t], z_recv.at[t], target))

    for copy in got_w:
        copy.wait()
    xs = []
    for c in range(chunks):
        got_x[c].wait()
        x = x_v[c * rows : (c + 1) * rows]
        masks = [column(types_ref[c * CHUNK + b : c * CHUNK + b + 1, :]) for b in range(CHUNK)]
        totals = [None] * CHUNK
        for kind in range(kinds):
            both = jnp.concatenate([wk_v[kind], wv_v[kind]], axis=1)
            out = jnp.dot(x, both, preferred_element_type=jnp.float32)
            for b in range(CHUNK):
                piece = out[b * block : (b + 1) * block]
                pair = (piece[:, :cols], piece[:, cols:])
                if totals[b] is None:
                    totals[b] = pair
                else:
                    hit = masks[b] == float(kind)
                    totals[b] = tuple(jnp.where(hit, new, old) for new, old in zip(pair, totals[b]))
        first = n * blocks + c * CHUNK
        for b in range(CHUNK):
            k_all[first + b] = totals[b][0].astype(bf)
            vt_all[first + b] = totals[b][1].T.astype(bf)
        for t in range(1, n_node):
            target = {"node": lax.rem(n + t, n_node)}
            for which, ref in enumerate((k_all, vt_all)):
                part = ref.at[pl.ds(first, CHUNK)]
                xs.append(send(part, part, x_send.at[t, c, which], x_recv.at[t, c, which], target))

    got_q.wait()
    wide = jnp.concatenate([wq_v[kind] for kind in range(kinds)], axis=1)
    mine = [own_block(d, per, n_rel, r) for d in range(own_blocks)]
    x = jnp.concatenate([x_v[pl.ds(pl.multiple_of(b * block, block), block)] for b in mine], axis=0)
    out = jnp.dot(x, wide, preferred_element_type=jnp.float32)
    for d in range(own_blocks):
        mask = column(types_ref[pl.ds(mine[d], 1), :])
        piece = out[d * block : (d + 1) * block]
        total = piece[:, :cols]
        for kind in range(1, kinds):
            total = jnp.where(mask == float(kind), piece[:, kind * cols : (kind + 1) * cols], total)
        qt_ref[d] = total.T.astype(bf)

    got_out.wait()
    os = []
    for i, t in enumerate(pairs):
        target = {"head": lax.rem(h + t, n_head)}
        os.append(send(w_all.at[h], w_all.at[h], o_send.at[i], o_recv.at[i], target))
    own_out = send(w_all.at[h], w_all.at[h], o_send.at[len(pairs)], o_recv.at[len(pairs)], {"head": sibling})

    def diagonal(ref, index):
        lines = []
        for k in range(heads):
            parts = [jnp.zeros((size, size), jnp.float32)] * heads
            parts[k] = ref[index, k].astype(jnp.float32)
            lines.append(jnp.concatenate(parts, axis=1))
        return jnp.concatenate(lines, axis=0)

    def relation(index, carry):
        att_out[index] = diagonal(att_v, index).astype(bf)
        msg_out[index] = diagonal(msg_v, index).T.astype(bf)
        return carry

    for copy in got_rel:
        copy.wait()
    ys, ds = [], []
    step = relations // n_rel
    for t in range(1, n_rel):
        lax.fori_loop((t - 1) * step, relations if t == n_rel - 1 else t * step, relation, 0)
        zs[t - 1].wait_recv()
        source = lax.rem(r + n_rel - t, n_rel)
        for i, u in enumerate(pairs):
            target = {"head": lax.rem(h + u, n_head)}
            ys.append((t, u, send(bit_rows(source, h), bit_rows(source, h), y_send.at[t, i], y_recv.at[t, i], target)))
        ds.append(
            send(bit_rows(source, h), bit_rows(source, h), d_send.at[t, 0], d_recv.at[t, 0], {"head": sibling})
        )

    for copy in metas:
        copy.wait_recv()
    used = slots // block
    meta = jnp.concatenate([meta_all[s, :used] for s in range(n_rel)], axis=0)
    compact(meta, own_blocks, per, n_rel, r, fields, list_ref)

    for i, (t, u, copy) in enumerate(ys):
        copy.wait_recv()
        source = lax.rem(r + n_rel - t, n_rel)
        head = lax.rem(h + n_head - u, n_head)
        which = 1 + pairs.index(u)
        ds.append(
            send(bit_rows(source, head), bit_rows(source, head), d_send.at[t, which], d_recv.at[t, which], {"head": sibling})
        )
    for i, t in enumerate(pairs):
        os[i].wait_recv()
        head = lax.rem(h + n_head - t, n_head)
        index = len(pairs) + 1 + i
        ds.append(send(w_all.at[head], w_all.at[head], o_send.at[index], o_recv.at[index], {"head": sibling}))
    own_out.wait_recv()
    for copy in ds:
        copy.wait_recv()
    for copy in xs:
        copy.wait_recv()
    for copy in started:
        copy.wait_send()


def tile_kernel(heads, factor, fields, list_ref, prior_ref, qt_ref, k_ref, vt_ref, bits_ref, att_ref, msg_ref, *refs):
    acc_ref, top_ref, left, right, scores, peak = refs
    src_bits, _, slot_bits, rel_bits, own_bits = fields
    own_blocks, cols, block = qt_ref.shape
    size = cols // heads
    words = bits_ref.shape[1]
    tall = acc_ref.shape[1]
    span = heads * block
    groups = list_ref[list_ref.shape[0] - 1, 0]

    acc_ref[...] = jnp.zeros_like(acc_ref)
    top_ref[...] = jnp.full_like(top_ref, FLOOR)
    right[...] = jnp.zeros_like(right)
    row = lax.broadcasted_iota(jnp.int32, (tall, span), 0)
    lane = lax.broadcasted_iota(jnp.int32, (tall, span), 1)
    ones = jnp.zeros((tall, span), jnp.float32)
    for k in range(heads):
        ones = jnp.where((row == cols + k) & (lane >= k * block) & (lane < (k + 1) * block), 1.0, ones)
    ones = ones.astype(jnp.bfloat16)
    for u in range(GROUP):
        left[:, u * span : (u + 1) * span] = ones
    bit_of = lax.shift_left(jnp.int32(1), lax.broadcasted_iota(jnp.int32, (32, block), 0))
    sum_row = lax.broadcasted_iota(jnp.int32, (tall - cols, block), 0)

    def entries(group):
        line = lax.shift_right_logical(group * GROUP, 7)
        start = (group * GROUP) & 127
        found = []
        for u in range(GROUP):
            value = list_ref[line, start + u]
            slot = value & ((1 << slot_bits) - 1)
            rest = lax.shift_right_logical(value, slot_bits)
            src = rest & ((1 << src_bits) - 1)
            rest = lax.shift_right_logical(rest, src_bits)
            rel = rest & ((1 << rel_bits) - 1)
            rest = lax.shift_right_logical(rest, rel_bits)
            dst = rest & ((1 << own_bits) - 1)
            valid = -lax.shift_right_logical(rest, own_bits)
            found.append((slot, src, rel, dst, valid))
        return found

    def turn(group):
        picks = entries(group)
        dst = picks[0][3]
        stack = jnp.concatenate([att_ref[rel] for _, _, rel, _, _ in picks], axis=0)
        turned = jnp.dot(stack, qt_ref[dst], preferred_element_type=jnp.float32)
        for u, (_, _, rel, _, _) in enumerate(picks):
            for k in range(heads):
                lo = u * cols + k * size
                scaled = turned[lo : lo + size] * (prior_ref[rel * heads + k] * factor)
                right[u, k * size : (k + 1) * size, k * block : (k + 1) * block] = scaled.astype(jnp.bfloat16)

    def send_messages(group):
        for u, (_, src, rel, _, _) in enumerate(entries(group)):
            message = jnp.dot(msg_ref[rel], vt_ref[src], preferred_element_type=jnp.float32).astype(jnp.bfloat16)
            for k in range(heads):
                lo = u * span + k * block
                left[k * size : (k + 1) * size, lo : lo + block] = message[k * size : (k + 1) * size]

    def score(group):
        best = [None] * heads
        for u, (slot, src, _, _, valid) in enumerate(entries(group)):
            found = jnp.dot(k_ref[src], right[u], preferred_element_type=jnp.float32)
            tile_words = bits_ref[slot] & valid
            edges = jnp.concatenate([(tile_words[w : w + 1] & bit_of) != 0 for w in range(words)], axis=0)
            for k in range(heads):
                masked = jnp.where(edges, found[:, k * block : (k + 1) * block], NEG)
                scores[u * heads + k] = masked
                top = jnp.max(masked.reshape(block // 8, 8, block), axis=0)
                best[k] = top if best[k] is None else jnp.maximum(best[k], top)
        for k in range(heads):
            peak[k : k + 1] = jnp.max(best[k], axis=0, keepdims=True)

    def gather(group):
        dst = entries(group)[0][3]
        keeps, weights = [], [None] * (GROUP * heads)
        for k in range(heads):
            old = top_ref[dst, k : k + 1]
            new = jnp.maximum(old, peak[k : k + 1])
            top_ref[dst, k : k + 1] = new
            keeps.append(jnp.exp(old - new))
            for u in range(GROUP):
                weights[u * heads + k] = jnp.exp(scores[u * heads + k] - new).astype(jnp.bfloat16)
        out = jnp.dot(left[...], jnp.concatenate(weights, axis=0), preferred_element_type=jnp.float32)
        for k in range(heads):
            rows = slice(k * size, (k + 1) * size)
            acc_ref[dst, rows] = acc_ref[dst, rows] * keeps[k] + out[rows]
        keep = jnp.broadcast_to(keeps[0], sum_row.shape)
        for k in range(1, heads):
            keep = jnp.where(sum_row == k, keeps[k], keep)
        acc_ref[dst, cols:] = acc_ref[dst, cols:] * keep + out[cols:]

    def visit(group, carry):
        gather(group)
        score(group + 1)
        send_messages(group + 1)
        turn(group + 2)
        return carry

    turn(0)
    score(0)
    send_messages(0)
    turn(1)
    lax.fori_loop(0, groups, visit, 0)


def finish_kernel(n_rel, n_head, heads, acc_ref, types_ref, skip_ref, feat_ref, w_ref, *refs):
    out_ref, hid_out, hid_got, resid, send_sem, recv_sem, local = refs
    own_blocks, _, block = acc_ref.shape
    kinds = w_ref.shape[1]
    cols = w_ref.shape[2]
    width = w_ref.shape[3]
    size = cols // heads
    per = own_blocks // n_head
    piece = per * block
    r = lax.axis_index("rel")
    h = lax.axis_index("head")
    span = n_rel * piece

    fetch = pltpu.make_async_copy(feat_ref.at[pl.ds(pl.multiple_of(h * span, span), span)], resid, local.at[0])
    fetch.start()
    barrier = pltpu.get_barrier_semaphore()
    shifts = [(a, b) for b in range(n_head) for a in range(n_rel) if a or b]
    for a, b in shifts:
        target = {"rel": lax.rem(r + a, n_rel), "head": lax.rem(h + b, n_head)}
        pl.semaphore_signal(barrier, inc=1, device_id=target)

    def hidden_of(source):
        total = jnp.maximum(acc_ref[source, cols : cols + 8], 1.0)
        sides = []
        for k in range(heads):
            sides.append(acc_ref[source, pl.ds(k * size, size)] / total[k : k + 1])
        agg = jnp.concatenate(sides, axis=0)
        inner = math.sqrt(2.0 / math.pi) * (agg + 0.044715 * (agg * agg * agg))
        hidden = agg * (0.5 * (1.0 + jnp.tanh(inner)))
        return hidden.T.astype(jnp.bfloat16)

    for b in range(n_head):
        head = lax.rem(h + b, n_head)
        for i in range(per):
            hid_out[b, i * block : (i + 1) * block] = hidden_of(head * per + i)
    pl.semaphore_wait(barrier, len(shifts))

    sends = {}
    for a, b in sorted(shifts, key=lambda s: (s[0] == 0, s[1])):
        target = {"rel": lax.rem(r + a, n_rel), "head": lax.rem(h + b, n_head)}
        copy = pltpu.make_async_remote_copy(
            src_ref=hid_out.at[b],
            dst_ref=hid_got.at[a, b],
            send_sem=send_sem.at[a, b],
            recv_sem=recv_sem.at[a, b],
            device_id=target,
        )
        copy.start()
        sends[a, b] = copy
    hid_got[0, 0] = hid_out[0]
    fetch.wait()
    gates = []
    for a in range(n_rel):
        source = lax.rem(r + n_rel - a, n_rel)
        for b in range(n_head):
            if a or b:
                sends[a, b].wait_recv()
        parts = [hid_got[a, lax.rem(h + n_head - head, n_head)] for head in range(n_head)]
        hidden = jnp.concatenate(parts, axis=1)
        outs = []
        for kind in range(kinds):
            weights = jnp.concatenate([w_ref[head, kind] for head in range(n_head)], axis=0)
            outs.append(jnp.dot(hidden, weights, preferred_element_type=jnp.float32))
        for i in range(per):
            mask = column(types_ref[pl.ds((h * n_rel + source) * per + i, 1), :])
            masks = [mask == float(kind) for kind in range(kinds)]
            logit = jnp.full((block, block), skip_ref[0], jnp.float32)
            for kind in range(1, kinds):
                logit = jnp.where(masks[kind], skip_ref[kind], logit)
            gate = 1.0 / (1.0 + jnp.exp(-logit))
            rows = pl.ds(pl.multiple_of(source * piece + i * block, block), block)
            for w in range(width // block):
                lanes = slice(w * block, (w + 1) * block)
                total = outs[0][i * block : (i + 1) * block, lanes]
                for kind in range(1, kinds):
                    total = jnp.where(masks[kind], outs[kind][i * block : (i + 1) * block, lanes], total)
                old = resid[rows, lanes].astype(jnp.float32)
                out_ref[rows, lanes] = (gate * total + (1.0 - gate) * old).astype(jnp.bfloat16)
    for copy in sends.values():
        copy.wait_send()


def per_device(
    features,
    node_type,
    w_query,
    w_key,
    w_value,
    rel_att,
    rel_msg,
    rel_prior,
    w_out,
    skip,
    rel_perm,
    tile_src,
    tile_dst,
    tile_bits,
    tile_count,
):
    node_rows, width = features.shape
    n_rel = lax.axis_size("rel")
    n_node = lax.axis_size("node")
    n_head = lax.axis_size("head")
    relations, heads = rel_prior.shape
    cols = w_query.shape[2]
    kinds = w_query.shape[0]
    block = tile_bits.shape[2]
    words = tile_bits.shape[3]
    blocks = node_rows // block
    positions, tcap = tile_src.shape
    slots = positions * tcap
    factor = 1.0 / math.sqrt(cols // heads)
    own_blocks = blocks // n_rel
    all_slots = n_rel * slots
    bf = jnp.bfloat16
    fields = (
        bits_for(n_node * blocks),
        bits_for(blocks),
        bits_for(all_slots),
        bits_for(relations),
        bits_for(own_blocks),
    )

    live = jnp.arange(tcap, dtype=jnp.int32)[None, :] < tile_count.reshape(positions, 1)
    packed = tile_src | (tile_dst << fields[0]) | (rel_perm[:, None] << (fields[0] + fields[1]))
    packed = jnp.where(live, packed, -1).reshape(slots // block, block)
    packed = jnp.pad(packed, ((0, 8 - slots // block), (0, 0)), constant_values=-1)
    bits = tile_bits.transpose(0, 1, 3, 2).reshape(slots, words, block)

    list_rows = -(-(all_slots + own_blocks * GROUP + 3 * GROUP) // block) + 1
    chunks = blocks // CHUNK
    half = max(n_head // 2 - 1, 1)
    dma = pltpu.SemaphoreType.DMA
    smem = pl.BlockSpec(memory_space=pltpu.SMEM)
    vmem = pl.BlockSpec(memory_space=pltpu.VMEM)
    hbm = pl.BlockSpec(memory_space=pl.ANY)
    shape = jax.ShapeDtypeStruct
    keys, values_t, query_t, att, msg, all_bits, all_out, listed = pl.pallas_call(
        functools.partial(prepare_kernel, n_rel, n_node, n_head, fields),
        in_specs=[vmem, vmem] + [hbm] * 8,
        out_specs=[vmem] * 8,
        out_shape=[
            shape((n_node * blocks, block, cols), bf),
            shape((n_node * blocks, cols, block), bf),
            shape((own_blocks, cols, block), bf),
            shape((relations, cols, cols), bf),
            shape((relations, cols, cols), bf),
            shape((all_slots, words, block), jnp.int32),
            shape((n_head,) + w_out.shape, bf),
            shape((list_rows, block), jnp.int32),
        ],
        scratch_shapes=[
            pltpu.VMEM(features.shape, bf),
            pltpu.VMEM(w_key.shape, bf),
            pltpu.VMEM(w_value.shape, bf),
            pltpu.VMEM(w_query.shape, bf),
            pltpu.VMEM(rel_att.shape, bf),
            pltpu.VMEM(rel_msg.shape, bf),
            pltpu.VMEM((n_rel, 8, block), jnp.int32),
            dma((8 + chunks,)),
            dma((n_rel,)),
            dma((n_rel,)),
            dma((n_rel, half)),
            dma((n_rel, half)),
            dma((n_rel, 1 + half)),
            dma((n_rel, 1 + half)),
            dma((n_rel,)),
            dma((n_rel,)),
            dma((n_node, chunks, 2)),
            dma((n_node, chunks, 2)),
            dma((n_head,)),
            dma((n_head,)),
        ],
        compiler_params=pltpu.CompilerParams(collective_id=0, has_side_effects=True, vmem_limit_bytes=VMEM_BYTES),
        name="prepare",
    )(packed, node_type.reshape(blocks, block), features, w_key, w_value, w_query, rel_att, rel_msg, w_out, bits)

    tall = cols + PAD_ROWS
    acc = pl.pallas_call(
        functools.partial(tile_kernel, heads, factor, fields),
        in_specs=[smem] * 2 + [vmem] * 6,
        out_specs=vmem,
        out_shape=shape((own_blocks, tall, block), jnp.float32),
        scratch_shapes=[
            pltpu.VMEM((own_blocks, 8, block), jnp.float32),
            pltpu.VMEM((tall, GROUP * heads * block), bf),
            pltpu.VMEM((GROUP, cols, heads * block), bf),
            pltpu.VMEM((GROUP * heads, block, block), jnp.float32),
            pltpu.VMEM((8, block), jnp.float32),
        ],
        compiler_params=pltpu.CompilerParams(vmem_limit_bytes=VMEM_BYTES),
        name="tiles",
    )(listed, rel_prior.reshape(-1), query_t, keys, values_t, all_bits, att, msg)

    piece = own_blocks // n_head * block
    return pl.pallas_call(
        functools.partial(finish_kernel, n_rel, n_head, heads),
        in_specs=[vmem, vmem, smem, hbm, vmem],
        out_specs=vmem,
        out_shape=shape((n_rel * piece, width), bf),
        scratch_shapes=[
            pltpu.VMEM((n_head, piece, cols), bf),
            pltpu.VMEM((n_rel, n_head, piece, cols), bf),
            pltpu.VMEM((n_rel * piece, width), bf),
            dma((n_rel, n_head)),
            dma((n_rel, n_head)),
            dma((1,)),
        ],
        compiler_params=pltpu.CompilerParams(collective_id=1, has_side_effects=True, vmem_limit_bytes=VMEM_BYTES),
        name="finish",
    )(acc, node_type.reshape(blocks, block), skip, features, all_out)


def solution(mesh):
    in_specs = (
        P("node", None),
        P("node"),
        P(None, None, "head"),
        P(None, None, "head"),
        P(None, None, "head"),
        P(None, "head", None, None),
        P(None, "head", None, None),
        P(None, "head"),
        P(None, "head", None),
        P(),
        P("rel"),
        P("rel", "node"),
        P("rel", "node"),
        P("rel", "node", None, None),
        P("rel", "node"),
    )
    out_specs = P(("node", "head"), None)
    return jax.shard_map(
        per_device, mesh=mesh, in_specs=in_specs, out_specs=out_specs, check_vma=False
    )
```

profile of v0, /device:TPU:1, one launch (start us, length us, event | category | flops | bytes accessed | tf_op | source)
XLA Modules:
  0.0 80.3 jit_solution(14096626526503508938)
XLA Ops:
  0.0 0.7 broadcast_shift-left_fusion
  0.7 0.8 or_select_fusion
  1.4 0.1 reshape.15
  1.5 0.8 copy.17
  2.3 0.1 reshape.18.prior_ref
  2.4 0.0 copy-start
  2.5 1.6 %copy-done = bf16[2048,512]{1,0:T(8,128)(2,1)S(1)} copy-done((bf16[2048,512]{1,0:T(8,128)(2,1)S(1)}, bf16[2048,512]{1,0:T(8,128)(2,1)}, u32[]{:S(2)}) %copy-start) | copy-done | bytes 2097176
  4.0 1.6 %copy-done.2 = bf16[64,2,64,64]{3,2,1,0:T(8,128)(2,1)S(1)} copy-done((bf16[64,2,64,64]{3,2,1,0:T(8,128)(2,1)S(1)}, bf16[64,2,64,64]{3,2,1,0:T(8,128)(2,1)}, u32[]{:S(2)}) %copy-start.2) | copy-done | bytes 1048600
  5.6 1.6 %copy-done.3 = bf16[64,2,64,64]{3,2,1,0:T(8,128)(2,1)S(1)} copy-done((bf16[64,2,64,64]{3,2,1,0:T(8,128)(2,1)S(1)}, bf16[64,2,64,64]{3,2,1,0:T(8,128)(2,1)}, u32[]{:S(2)}) %copy-start.3) | copy-done | bytes 1048600
  7.2 1.0 %copy-done.4 = bf16[4,512,128]{2,1,0:T(8,128)(2,1)S(1)} copy-done((bf16[4,512,128]{2,1,0:T(8,128)(2,1)S(1)}, bf16[4,512,128]{2,1,0:T(8,128)(2,1)}, u32[]{:S(2)}) %copy-start.4) | copy-done | bytes 524312
  8.3 1.0 %copy-done.5 = bf16[4,512,128]{2,1,0:T(8,128)(2,1)S(1)} copy-done((bf16[4,512,128]{2,1,0:T(8,128)(2,1)S(1)}, bf16[4,512,128]{2,1,0:T(8,128)(2,1)}, u32[]{:S(2)}) %copy-start.5) | copy-done | bytes 524312
  9.3 1.0 %copy-done.6 = bf16[4,512,128]{2,1,0:T(8,128)(2,1)S(1)} copy-done((bf16[4,512,128]{2,1,0:T(8,128)(2,1)S(1)}, bf16[4,512,128]{2,1,0:T(8,128)(2,1)}, u32[]{:S(2)}) %copy-start.6) | copy-done | bytes 524312
  10.4 1.0 %copy-done.7 = bf16[4,128,512]{2,1,0:T(8,128)(2,1)S(1)} copy-done((bf16[4,128,512]{2,1,0:T(8,128)(2,1)S(1)}, bf16[4,128,512]{2,1,0:T(8,128)(2,1)}, u32[]{:S(2)}) %copy-start.7) | copy-done | bytes 524312
  11.4 1.0 %copy-done.8 = s32[16,16,128,4]{2,3,1,0:T(4,128)S(1)} copy-done((s32[16,16,128,4]{2,3,1,0:T(4,128)S(1)}, s32[16,16,128,4]{2,3,1,0:T(4,128)}, u32[]{:S(2)}) %copy-start.8) | copy-done | bytes 524312
  12.4 0.7 copy-done.9
  13.1 33.6 %prepare.1 = (bf16[32,128,128]{2,1,0:T(8,128)(2,1)S(1)}, bf16[32,128,128]{2,1,0:T(8,128)(2,1)S(1)}, bf16[4,128,128]{2,1,0:T(8,128)(2,1)S(1)}, bf16[64,128,128]{2...) custom-call(s32[8,128]{1,0:T(8,128)S(1)} %pad.4.refs_0_, ...), custom_call_target="tpu_custom_call" | custom-call | tf_op jit(solution)/shard_map/prepare/pallas_call | solution.py:514
  46.8 0.0 copy-start.1
  46.8 0.0 copy-start.10
  46.8 0.0 copy-start.11
  46.8 15.6 %tiles.1.acc_ref = f32[4,144,128]{2,1,0:T(8,128)S(1)} custom-call(s32[10,128]{1,0:T(8,128)S(1)} %get-tuple-element.13.list_ref, f32[128]{0:T(128)S(1)} %reshape.18.prior_ref, bf16[4,128,128]{2,1,0:T(8,128)(2,1)S(1)} %get-tuple-element.14.qt_ref, bf16[32,128,128]{2,1,0:T(8,128)(2,1)S(1)} %get-tuple-element.15.k_ref, ...), custom_call_target="tpu_custom_call" | custom-call | tf_op jit(solution)/shard_map/tiles/pallas_call | solution.py:555
  62.4 0.0 copy-done.1
  62.4 0.0 copy-done.10
  62.4 17.1 %finish.1 = bf16[512,512]{1,0:T(8,128)(2,1)S(1)} custom-call(f32[4,144,128]{2,1,0:T(8,128)S(1)} %tiles.1.acc_ref, s32[16,128]{1,0:T(8,128)S(1)} %bitcast.7, f32[4]{0:T(128)S(1)} %copy-done.11, bf16[2048,512]{1,0:T(8,128)(2,1)S(1)} %copy-done.1, bf16[4,4,128,512]{3,2,1,0:T(8,128)(2,1)S(1)} %get-tuple-element.20.w_ref), custom_call_target="tpu_custom_call" | custom-call | tf_op jit(solution)/shard_map/finish/pallas_call | solution.py:572
  79.5 0.8 copy.19
  (10 shorter events, 0.0 us)
Async XLA Ops:
  2.4 1.6 %copy-start = (bf16[2048,512]{1,0:T(8,128)(2,1)S(1)}, bf16[2048,512]{1,0:T(8,128)(2,1)}, u32[]{:S(2)}) copy-start(bf16[2048,512]{1,0:T(8,128)(2,1)} %feat_ref.1) | copy-start | bytes 6291460
  4.0 1.6 %copy-start.2 = (bf16[64,2,64,64]{3,2,1,0:T(8,128)(2,1)S(1)}, bf16[64,2,64,64]{3,2,1,0:T(8,128)(2,1)}, u32[]{:S(2)}) copy-start(bf16[64,2,64,64]{3,2,1,0:T(8,128)(2,1)} %refs_6_.1) | copy-start | bytes 3145732
  5.6 1.6 %copy-start.3 = (bf16[64,2,64,64]{3,2,1,0:T(8,128)(2,1)S(1)}, bf16[64,2,64,64]{3,2,1,0:T(8,128)(2,1)}, u32[]{:S(2)}) copy-start(bf16[64,2,64,64]{3,2,1,0:T(8,128)(2,1)} %refs_7_.1) | copy-start | bytes 3145732
  7.2 1.0 %copy-start.4 = (bf16[4,512,128]{2,1,0:T(8,128)(2,1)S(1)}, bf16[4,512,128]{2,1,0:T(8,128)(2,1)}, u32[]{:S(2)}) copy-start(bf16[4,512,128]{2,1,0:T(8,128)(2,1)} %refs_3_.1) | copy-start | bytes 1572868
  8.3 1.0 %copy-start.5 = (bf16[4,512,128]{2,1,0:T(8,128)(2,1)S(1)}, bf16[4,512,128]{2,1,0:T(8,128)(2,1)}, u32[]{:S(2)}) copy-start(bf16[4,512,128]{2,1,0:T(8,128)(2,1)} %refs_4_.1) | copy-start | bytes 1572868
  9.3 1.0 %copy-start.6 = (bf16[4,512,128]{2,1,0:T(8,128)(2,1)S(1)}, bf16[4,512,128]{2,1,0:T(8,128)(2,1)}, u32[]{:S(2)}) copy-start(bf16[4,512,128]{2,1,0:T(8,128)(2,1)} %refs_5_.1) | copy-start | bytes 1572868
  10.4 1.0 %copy-start.7 = (bf16[4,128,512]{2,1,0:T(8,128)(2,1)S(1)}, bf16[4,128,512]{2,1,0:T(8,128)(2,1)}, u32[]{:S(2)}) copy-start(bf16[4,128,512]{2,1,0:T(8,128)(2,1)} %refs_8_.1) | copy-start | bytes 1572868
  11.4 1.0 %copy-start.8 = (s32[16,16,128,4]{2,3,1,0:T(4,128)S(1)}, s32[16,16,128,4]{2,3,1,0:T(4,128)}, u32[]{:S(2)}) copy-start(s32[16,16,128,4]{2,3,1,0:T(4,128)} %param.28) | copy-start | bytes 1572868
  12.4 0.7 copy-start.9
  46.8 15.6 %copy-start.1 = (bf16[2048,512]{1,0:T(8,128)(2,1)S(1)}, bf16[2048,512]{1,0:T(8,128)(2,1)}, u32[]{:S(2)}) copy-start(bf16[2048,512]{1,0:T(8,128)(2,1)} %feat_ref.1) | copy-start | bytes 6291460
  46.8 15.6 %copy-start.10 = (s32[2048]{0:T(1024)S(1)}, s32[2048]{0:T(1024)}, u32[]{:S(2)}) copy-start(s32[2048]{0:T(1024)} %param.16) | copy-start | bytes 24580
  46.8 15.6 %copy-start.11 = (f32[4]{0:T(128)S(1)}, f32[4]{0:T(128)}, u32[]{:S(2)}) copy-start(f32[4]{0:T(128)} %skip_ref.1) | copy-start | bytes 52
where the time goes:
time: 80 us; the launch traced here: 80.3 us
  Pallas kernels  66.3 us (83%)
  local copies, waits for them, and re-layouts  12.5 us (16%)
  other arithmetic  1.44 us (2%)
    pallas_call x1, Pallas kernels, per_device(): pl.pallas_call(functools.partial(prepare_kernel, n_rel, n_node, n_head, f...  33.6 us
    pallas_call x1, Pallas kernels, per_device(): pl.pallas_call(functools.partial(finish_kernel, n_rel, n_head, heads), in...  17.1 us
    pallas_call x1, Pallas kernels, per_device(): pl.pallas_call(functools.partial(tile_kernel, heads, factor, fields), in_...  15.6 us
    unnamed x26, local copies, waits for them, and re-layouts  12.3 us

commit v1 on v0

--- a/solution.py
+++ b/solution.py
@@ -19,6 +19,10 @@
 def column(types_row):
     size = types_row.shape[1]
     return jnp.broadcast_to(types_row.astype(jnp.float32), (size, size)).T
+
+
+def in_hbm(value):
+    return pltpu.with_memory_space_constraint(value, pltpu.HBM)
 
 
 def bits_for(count):
@@ -93,11 +97,34 @@
     list_ref[list_ref.shape[0] - 1 :] = groups
 
 
+def pack(src, dst, count, perm, fields, lanes):
+    positions, tcap = src.shape
+    i = lax.broadcasted_iota(jnp.int32, (positions, positions), 0)
+    j = lax.broadcasted_iota(jnp.int32, (positions, positions), 1)
+
+    def upright(row):
+        return jnp.sum(jnp.where(i == j, row.astype(jnp.float32), 0.0), axis=1, keepdims=True).astype(jnp.int32)
+
+    word = src | lax.shift_left(dst, fields[0]) | lax.shift_left(upright(perm), fields[0] + fields[1])
+    slot = lax.broadcasted_iota(jnp.int32, src.shape, 1)
+    word = jnp.where(slot < upright(count), word, -1)
+    each = lanes // tcap
+    rows = [
+        jnp.concatenate([word[a + b : a + b + 1] for b in range(each)], axis=1) for a in range(0, positions, each)
+    ]
+    rows.append(jnp.full((8 - len(rows), lanes), -1, jnp.int32))
+    return jnp.concatenate(rows, axis=0).reshape(1, 8, lanes)
+
+
 def prepare_kernel(n_rel, n_node, n_head, fields, *refs):
-    (packed_ref, types_ref, feat_ref, wk_ref, wv_ref, wq_ref, att_ref, msg_ref, wout_ref, bits_ref) = refs[:10]
-    (k_all, vt_all, qt_ref, att_out, msg_out, bits_all, w_all, list_ref) = refs[10:18]
-    (x_v, wk_v, wv_v, wq_v, att_v, msg_v, meta_all) = refs[18:25]
-    (local, z_send, z_recv, y_send, y_recv, d_send, d_recv, m_send, m_recv, x_send, x_recv, o_send, o_recv) = refs[25:]
+    (small, feat_ref, wk_ref, wv_ref, wq_ref, att_ref, msg_ref, wout_ref, bits_ref), refs = (
+        (refs[:5],) + refs[5:13],
+        refs[13:],
+    )
+    (k_all, vt_all, qt_ref, att_out, msg_out, bits_all, w_all, list_ref) = refs[:8]
+    (x_v, wk_v, wv_v, wq_v, att_v, msg_v, meta_all), refs = refs[8:15], refs[15:]
+    (types_ref, src_v, dst_v, count_v, perm_v), refs = refs[:5], refs[5:]
+    (local, z_send, z_recv, y_send, y_recv, d_send, d_recv, m_send, m_recv, x_send, x_recv, o_send, o_recv) = refs
     blocks = types_ref.shape[0]
     block = types_ref.shape[1]
     cols = wk_v.shape[2]
@@ -121,6 +148,8 @@
         copy.start()
         return copy
 
+    small_v = (types_ref, src_v, dst_v, count_v, perm_v)
+    got_small = [fetch(a, b, 8 + chunks + i) for i, (a, b) in enumerate(zip(small, small_v))]
     own_bits = fetch(bits_ref, bits_all.at[pl.ds(pl.multiple_of(r * slots, slots), slots)], 0)
     got_w = [fetch(wk_ref, wk_v, 1), fetch(wv_ref, wv_v, 2)]
     got_x = []
@@ -138,7 +167,9 @@
     for t in pairs:
         pl.semaphore_signal(barrier, inc=1, device_id={"head": lax.rem(h + t, n_head)})
     pl.semaphore_signal(barrier, inc=1, device_id={"head": sibling})
-    meta_all[pl.ds(r, 1)] = packed_ref[...].reshape((1,) + packed_ref.shape)
+    for copy in got_small:
+        copy.wait()
+    meta_all[pl.ds(r, 1)] = pack(src_v[...], dst_v[...], count_v[...], perm_v[...], fields, block)
     pl.semaphore_wait(barrier, n_rel - 1 + n_node - 1 + len(pairs) + 1)
 
     started = []
@@ -317,7 +348,7 @@
         for u, (_, _, rel, _, _) in enumerate(picks):
             for k in range(heads):
                 lo = u * cols + k * size
-                scaled = turned[lo : lo + size] * (prior_ref[rel * heads + k] * factor)
+                scaled = turned[lo : lo + size] * (prior_ref[k, rel] * factor)
                 right[u, k * size : (k + 1) * size, k * block : (k + 1) * block] = scaled.astype(jnp.bfloat16)
 
     def send_messages(group):
@@ -497,10 +528,6 @@
         bits_for(own_blocks),
     )
 
-    live = jnp.arange(tcap, dtype=jnp.int32)[None, :] < tile_count.reshape(positions, 1)
-    packed = tile_src | (tile_dst << fields[0]) | (rel_perm[:, None] << (fields[0] + fields[1]))
-    packed = jnp.where(live, packed, -1).reshape(slots // block, block)
-    packed = jnp.pad(packed, ((0, 8 - slots // block), (0, 0)), constant_values=-1)
     bits = tile_bits.transpose(0, 1, 3, 2).reshape(slots, words, block)
 
     list_rows = -(-(all_slots + own_blocks * GROUP + 3 * GROUP) // block) + 1
@@ -509,11 +536,26 @@
     dma = pltpu.SemaphoreType.DMA
     smem = pl.BlockSpec(memory_space=pltpu.SMEM)
     vmem = pl.BlockSpec(memory_space=pltpu.VMEM)
-    hbm = pl.BlockSpec(memory_space=pl.ANY)
+    hbm = pl.BlockSpec(memory_space=pltpu.HBM)
     shape = jax.ShapeDtypeStruct
+    operands = (
+        node_type.reshape(blocks, block),
+        tile_src,
+        tile_dst,
+        tile_count.reshape(1, positions),
+        rel_perm.reshape(1, positions),
+        features,
+        w_key,
+        w_value,
+        w_query,
+        rel_att,
+        rel_msg,
+        w_out,
+        bits,
+    )
     keys, values_t, query_t, att, msg, all_bits, all_out, listed = pl.pallas_call(
         functools.partial(prepare_kernel, n_rel, n_node, n_head, fields),
-        in_specs=[vmem, vmem] + [hbm] * 8,
+        in_specs=[hbm] * 13,
         out_specs=[vmem] * 8,
         out_shape=[
             shape((n_node * blocks, block, cols), bf),
@@ -533,7 +575,12 @@
             pltpu.VMEM(rel_att.shape, bf),
             pltpu.VMEM(rel_msg.shape, bf),
             pltpu.VMEM((n_rel, 8, block), jnp.int32),
-            dma((8 + chunks,)),
+            pltpu.VMEM((blocks, block), jnp.int32),
+            pltpu.VMEM((positions, tcap), jnp.int32),
+            pltpu.VMEM((positions, tcap), jnp.int32),
+            pltpu.VMEM((1, positions), jnp.int32),
+            pltpu.VMEM((1, positions), jnp.int32),
+            dma((13 + chunks,)),
             dma((n_rel,)),
             dma((n_rel,)),
             dma((n_rel, half)),
@@ -549,7 +596,7 @@
         ],
         compiler_params=pltpu.CompilerParams(collective_id=0, has_side_effects=True, vmem_limit_bytes=VMEM_BYTES),
         name="prepare",
-    )(packed, node_type.reshape(blocks, block), features, w_key, w_value, w_query, rel_att, rel_msg, w_out, bits)
+    )(*[in_hbm(value) for value in operands])
 
     tall = cols + PAD_ROWS
     acc = pl.pallas_call(
@@ -566,7 +613,7 @@
         ],
         compiler_params=pltpu.CompilerParams(vmem_limit_bytes=VMEM_BYTES),
         name="tiles",
-    )(listed, rel_prior.reshape(-1), query_t, keys, values_t, all_bits, att, msg)
+    )(listed, rel_prior.T, query_t, keys, values_t, all_bits, att, msg)
 
     piece = own_blocks // n_head * block
     return pl.pallas_call(
@@ -584,7 +631,7 @@
         ],
         compiler_params=pltpu.CompilerParams(collective_id=1, has_side_effects=True, vmem_limit_bytes=VMEM_BYTES),
         name="finish",
-    )(acc, node_type.reshape(blocks, block), skip, features, all_out)
+    )(acc, node_type.reshape(blocks, block), skip, in_hbm(features), all_out)
 
 
 def solution(mesh):

time: 80 us -> 66.1 us (0.83)
  local copies, waits for them, and re-layouts: 12.5 us -> 0.81 us
  Pallas kernels: 66.3 us -> 64.8 us
  other arithmetic: 1.44 us -> 0 us
    unnamed x26 -> x7, local copies, waits for them, and re-layouts: 12.3 us -> 0.81 us
where the time goes in v1:
time: 66.1 us; the launch traced here: 65.7 us
  Pallas kernels  64.8 us (98%)
  local copies, waits for them, and re-layouts  0.81 us (1%)
    pallas_call x1, Pallas kernels, per_device(): pl.pallas_call(functools.partial(prepare_kernel, n_rel, n_node, n_head, f...  33.1 us
    pallas_call x1, Pallas kernels, per_device(): pl.pallas_call(functools.partial(finish_kernel, n_rel, n_head, heads), in...  17 us
    pallas_call x1, Pallas kernels, per_device(): pl.pallas_call(functools.partial(tile_kernel, heads, factor, fields), in_...  14.8 us

profile of v1, /device:TPU:1, one launch (start us, length us, event | category | flops | bytes accessed | tf_op | source)
XLA Modules:
  0.0 65.7 jit_solution(8808081968786640159)
XLA Ops:
  0.0 0.0 copy-start.1
  0.0 33.1 %prepare.1 = (bf16[32,128,128]{2,1,0:T(8,128)(2,1)S(1)}, bf16[32,128,128]{2,1,0:T(8,128)(2,1)S(1)}, bf16[4,128,128]{2,1,0:T(8,128)(2,1)S(1)}, bf16[64,128,128]{2...) custom-call(s32[16,128]{1,0:T(8,128)} %bitcast.7, ...), custom_call_target="tpu_custom_call" | custom-call | tf_op jit(solution)/shard_map/prepare/pallas_call | solution.py:556
  33.1 0.0 copy-done.1
  33.1 0.0 copy-start
  33.1 0.0 copy-start.2
  33.1 14.8 %tiles.1.acc_ref = f32[4,144,128]{2,1,0:T(8,128)S(1)} custom-call(s32[10,128]{1,0:T(8,128)S(1)} %get-tuple-element.13.list_ref, f32[2,64]{1,0:T(2,128)S(1)} %bitcast.9, bf16[4,128,128]{2,1,0:T(8,128)(2,1)S(1)} %get-tuple-element.14.qt_ref, bf16[32,128,128]{2,1,0:T(8,128)(2,1)S(1)} %get-tuple-element.15.k_ref, ...), custom_call_target="tpu_custom_call" | custom-call | tf_op jit(solution)/shard_map/tiles/pallas_call | solution.py:602
  47.9 0.0 copy-done
  47.9 0.0 copy-done.2
  47.9 17.0 %finish.1 = bf16[512,512]{1,0:T(8,128)(2,1)S(1)} custom-call(f32[4,144,128]{2,1,0:T(8,128)S(1)} %tiles.1.acc_ref, s32[16,128]{1,0:T(8,128)S(1)} %bitcast.8, f32[4]{0:T(128)S(1)} %copy-done.2, bf16[2048,512]{1,0:T(8,128)(2,1)} %feat_ref.1, bf16[4,4,128,512]{3,2,1,0:T(8,128)(2,1)S(1)} %get-tuple-element.20.w_ref), custom_call_target="tpu_custom_call" | custom-call | tf_op jit(solution)/shard_map/finish/pallas_call | solution.py:619
  64.9 0.8 %copy.17 = bf16[512,512]{1,0:T(8,128)(2,1)} copy(bf16[512,512]{1,0:T(8,128)(2,1)S(1)} %finish.1) | data formatting | bytes 1048576
Async XLA Ops:
  0.0 33.1 %copy-start.1 = (f32[64,2]{0,1:T(2,128)S(1)}, f32[64,2]{0,1:T(2,128)}, u32[]{:S(2)}) copy-start(f32[64,2]{0,1:T(2,128)} %param.22) | copy-start | bytes 1540
  33.1 14.8 %copy-start = (s32[2048]{0:T(1024)S(1)}, s32[2048]{0:T(1024)}, u32[]{:S(2)}) copy-start(s32[2048]{0:T(1024)} %param.16) | copy-start | bytes 24580
  33.1 14.8 %copy-start.2 = (f32[4]{0:T(128)S(1)}, f32[4]{0:T(128)}, u32[]{:S(2)}) copy-start(f32[4]{0:T(128)} %skip_ref.1) | copy-start | bytes 52

commit v2 on v1

--- a/solution.py
+++ b/solution.py
@@ -12,6 +12,8 @@
 FLOOR = -1e29
 GROUP = 4
 CHUNK = 4
+SPLIT = 3
+BATCH = 8
 PAD_ROWS = 16
 VMEM_BYTES = 30 * 1024 * 1024
 
@@ -117,14 +119,14 @@
 
 
 def prepare_kernel(n_rel, n_node, n_head, fields, *refs):
-    (small, feat_ref, wk_ref, wv_ref, wq_ref, att_ref, msg_ref, wout_ref, bits_ref), refs = (
-        (refs[:5],) + refs[5:13],
-        refs[13:],
+    (small, feat_ref, wk_ref, wv_ref, wq_ref, msg_ref, bits_ref), refs = (
+        (refs[:5],) + refs[5:11],
+        refs[11:],
     )
-    (k_all, vt_all, qt_ref, att_out, msg_out, bits_all, w_all, list_ref) = refs[:8]
-    (x_v, wk_v, wv_v, wq_v, att_v, msg_v, meta_all), refs = refs[8:15], refs[15:]
+    (kv_all, qt_ref, msg_out, bits_all, list_ref) = refs[:5]
+    (x_v, wk_v, wv_v, wq_v, msg_v, meta_all), refs = refs[5:11], refs[11:]
     (types_ref, src_v, dst_v, count_v, perm_v), refs = refs[:5], refs[5:]
-    (local, z_send, z_recv, y_send, y_recv, d_send, d_recv, m_send, m_recv, x_send, x_recv, o_send, o_recv) = refs
+    (local, z_send, z_recv, y_send, y_recv, d_send, d_recv, m_send, m_recv, x_send, x_recv, f_send, f_recv) = refs
     blocks = types_ref.shape[0]
     block = types_ref.shape[1]
     cols = wk_v.shape[2]
@@ -135,11 +137,13 @@
     per = own_blocks // n_head
     chunks = blocks // CHUNK
     rows = CHUNK * block
-    relations, heads, size = att_v.shape[0], att_v.shape[1], att_v.shape[2]
+    relations, heads, size = msg_v.shape[:3]
     r = lax.axis_index("rel")
     n = lax.axis_index("node")
     h = lax.axis_index("head")
     sibling = h + 1 - 2 * lax.rem(h, 2)
+    parity = lax.rem(r, 2)
+    partner = r + 1 - 2 * parity
     pairs = list(range(2, n_head, 2))
     bf = jnp.bfloat16
 
@@ -156,8 +160,7 @@
     for c in range(chunks):
         got_x.append(fetch(feat_ref.at[pl.ds(c * rows, rows)], x_v.at[pl.ds(c * rows, rows)], 8 + c))
     got_q = fetch(wq_ref, wq_v, 3)
-    got_rel = [fetch(att_ref, att_v, 4), fetch(msg_ref, msg_v, 5)]
-    got_out = fetch(wout_ref, w_all.at[h], 6)
+    got_rel = fetch(msg_ref, msg_v, 4)
 
     barrier = pltpu.get_barrier_semaphore()
     for t in range(1, n_rel):
@@ -196,7 +199,7 @@
 
     for copy in got_w:
         copy.wait()
-    xs = []
+    xs, halves = [], []
     for c in range(chunks):
         got_x[c].wait()
         x = x_v[c * rows : (c + 1) * rows]
@@ -215,13 +218,25 @@
                     totals[b] = tuple(jnp.where(hit, new, old) for new, old in zip(pair, totals[b]))
         first = n * blocks + c * CHUNK
         for b in range(CHUNK):
-            k_all[first + b] = totals[b][0].astype(bf)
-            vt_all[first + b] = totals[b][1].T.astype(bf)
+            kv_all[0, first + b] = totals[b][0].astype(bf)
+            kv_all[1, first + b] = totals[b][1].T.astype(bf)
         for t in range(1, n_node):
             target = {"node": lax.rem(n + t, n_node)}
-            for which, ref in enumerate((k_all, vt_all)):
-                part = ref.at[pl.ds(first, CHUNK)]
-                xs.append(send(part, part, x_send.at[t, c, which], x_recv.at[t, c, which], target))
+            if c < SPLIT:
+                part = kv_all.at[parity, pl.ds(first, CHUNK)]
+                halves.append((t, c, send(part, part, x_send.at[t, c, 0], x_recv.at[t, c, 0], target)))
+            else:
+                for which in range(2):
+                    part = kv_all.at[which, pl.ds(first, CHUNK)]
+                    xs.append(send(part, part, x_send.at[t, c, which], x_recv.at[t, c, which], target))
+
+    def forward(chunk):
+        for t, c, copy in halves:
+            if c == chunk:
+                copy.wait_recv()
+                first = lax.rem(n + n_node - t, n_node) * blocks + c * CHUNK
+                part = kv_all.at[parity, pl.ds(first, CHUNK)]
+                xs.append(send(part, part, f_send.at[t, c], f_recv.at[t, c], {"rel": partner}))
 
     got_q.wait()
     wide = jnp.concatenate([wq_v[kind] for kind in range(kinds)], axis=1)
@@ -236,32 +251,23 @@
             total = jnp.where(mask == float(kind), piece[:, kind * cols : (kind + 1) * cols], total)
         qt_ref[d] = total.T.astype(bf)
 
-    got_out.wait()
-    os = []
-    for i, t in enumerate(pairs):
-        target = {"head": lax.rem(h + t, n_head)}
-        os.append(send(w_all.at[h], w_all.at[h], o_send.at[i], o_recv.at[i], target))
-    own_out = send(w_all.at[h], w_all.at[h], o_send.at[len(pairs)], o_recv.at[len(pairs)], {"head": sibling})
-
-    def diagonal(ref, index):
-        lines = []
-        for k in range(heads):
-            parts = [jnp.zeros((size, size), jnp.float32)] * heads
-            parts[k] = ref[index, k].astype(jnp.float32)
-            lines.append(jnp.concatenate(parts, axis=1))
-        return jnp.concatenate(lines, axis=0)
+    got_rel.wait()
+    unit = lax.broadcasted_iota(jnp.int32, (size, size), 0) == lax.broadcasted_iota(jnp.int32, (size, size), 1)
+    unit = jnp.where(unit, 1.0, 0.0).astype(bf)
+    owner = lax.broadcasted_iota(jnp.int32, (size, cols), 1) // size
 
     def relation(index, carry):
-        att_out[index] = diagonal(att_v, index).astype(bf)
-        msg_out[index] = diagonal(msg_v, index).T.astype(bf)
+        flat = msg_v[pl.ds(index * BATCH, BATCH)].reshape(BATCH * cols, size)
+        turned = lax.dot_general(unit, flat, (((1,), (1,)), ((), ())), preferred_element_type=jnp.float32)
+        for i in range(BATCH):
+            both = turned[:, i * cols : (i + 1) * cols]
+            for k in range(heads):
+                part = jnp.where(owner == k, both, 0.0).astype(bf)
+                msg_out[index * BATCH + i, k * size : (k + 1) * size] = part
         return carry
 
-    for copy in got_rel:
-        copy.wait()
     ys, ds = [], []
-    step = relations // n_rel
     for t in range(1, n_rel):
-        lax.fori_loop((t - 1) * step, relations if t == n_rel - 1 else t * step, relation, 0)
         zs[t - 1].wait_recv()
         source = lax.rem(r + n_rel - t, n_rel)
         for i, u in enumerate(pairs):
@@ -270,14 +276,19 @@
         ds.append(
             send(bit_rows(source, h), bit_rows(source, h), d_send.at[t, 0], d_recv.at[t, 0], {"head": sibling})
         )
-
-    for copy in metas:
-        copy.wait_recv()
-    used = slots // block
-    meta = jnp.concatenate([meta_all[s, :used] for s in range(n_rel)], axis=0)
-    compact(meta, own_blocks, per, n_rel, r, fields, list_ref)
-
-    for i, (t, u, copy) in enumerate(ys):
+        if t == 1:
+            lax.fori_loop(0, relations // BATCH, relation, 0)
+            for copy in metas:
+                copy.wait_recv()
+            used = slots // block
+            meta = jnp.concatenate([meta_all[s, :used] for s in range(n_rel)], axis=0)
+            compact(meta, own_blocks, per, n_rel, r, fields, list_ref)
+        if t - 1 < SPLIT:
+            forward(t - 1)
+
+    for c in range(n_rel - 1, SPLIT):
+        forward(c)
+    for t, u, copy in ys:
         copy.wait_recv()
         source = lax.rem(r + n_rel - t, n_rel)
         head = lax.rem(h + n_head - u, n_head)
@@ -285,12 +296,6 @@
         ds.append(
             send(bit_rows(source, head), bit_rows(source, head), d_send.at[t, which], d_recv.at[t, which], {"head": sibling})
         )
-    for i, t in enumerate(pairs):
-        os[i].wait_recv()
-        head = lax.rem(h + n_head - t, n_head)
-        index = len(pairs) + 1 + i
-        ds.append(send(w_all.at[head], w_all.at[head], o_send.at[index], o_recv.at[index], {"head": sibling}))
-    own_out.wait_recv()
     for copy in ds:
         copy.wait_recv()
     for copy in xs:
@@ -299,29 +304,26 @@
         copy.wait_send()
 
 
-def tile_kernel(heads, factor, fields, list_ref, prior_ref, qt_ref, k_ref, vt_ref, bits_ref, att_ref, msg_ref, *refs):
-    acc_ref, top_ref, left, right, scores, peak = refs
+def tile_kernel(heads, factor, fields, list_ref, prior_ref, qt_ref, kv_ref, bits_ref, att_ref, msg_ref, *refs):
+    acc_ref, top_ref = refs[:2]
+    lefts, rights, scoress, peaks = refs[2:4], refs[4:6], refs[6:8], refs[8:10]
     src_bits, _, slot_bits, rel_bits, own_bits = fields
     own_blocks, cols, block = qt_ref.shape
     size = cols // heads
     words = bits_ref.shape[1]
-    tall = acc_ref.shape[1]
-    span = heads * block
+    tall = acc_ref.shape[2]
     groups = list_ref[list_ref.shape[0] - 1, 0]
 
     acc_ref[...] = jnp.zeros_like(acc_ref)
     top_ref[...] = jnp.full_like(top_ref, FLOOR)
-    right[...] = jnp.zeros_like(right)
-    row = lax.broadcasted_iota(jnp.int32, (tall, span), 0)
-    lane = lax.broadcasted_iota(jnp.int32, (tall, span), 1)
-    ones = jnp.zeros((tall, span), jnp.float32)
-    for k in range(heads):
-        ones = jnp.where((row == cols + k) & (lane >= k * block) & (lane < (k + 1) * block), 1.0, ones)
-    ones = ones.astype(jnp.bfloat16)
-    for u in range(GROUP):
-        left[:, u * span : (u + 1) * span] = ones
+    for right in rights:
+        right[...] = jnp.zeros_like(right)
+    row = lax.broadcasted_iota(jnp.int32, (tall - size, GROUP * block), 0)
+    ones = jnp.where(row == 0, 1.0, 0.0).astype(jnp.bfloat16)
+    for left in lefts:
+        for k in range(heads):
+            left[k, size:] = ones
     bit_of = lax.shift_left(jnp.int32(1), lax.broadcasted_iota(jnp.int32, (32, block), 0))
-    sum_row = lax.broadcasted_iota(jnp.int32, (tall - cols, block), 0)
 
     def entries(group):
         line = lax.shift_right_logical(group * GROUP, 7)
@@ -340,74 +342,86 @@
             found.append((slot, src, rel, dst, valid))
         return found
 
-    def turn(group):
-        picks = entries(group)
+    def turned_of(picks):
         dst = picks[0][3]
-        stack = jnp.concatenate([att_ref[rel] for _, _, rel, _, _ in picks], axis=0)
-        turned = jnp.dot(stack, qt_ref[dst], preferred_element_type=jnp.float32)
+        found = []
+        for k in range(heads):
+            stack = jnp.concatenate([att_ref[rel, k] for _, _, rel, _, _ in picks], axis=0)
+            query = qt_ref[dst, k * size : (k + 1) * size]
+            found.append(jnp.dot(stack, query, preferred_element_type=jnp.float32))
+        return found
+
+    def keep_turned(picks, turned, right):
         for u, (_, _, rel, _, _) in enumerate(picks):
             for k in range(heads):
-                lo = u * cols + k * size
-                scaled = turned[lo : lo + size] * (prior_ref[k, rel] * factor)
+                scaled = turned[k][u * size : (u + 1) * size] * (prior_ref[k, rel] * factor)
                 right[u, k * size : (k + 1) * size, k * block : (k + 1) * block] = scaled.astype(jnp.bfloat16)
 
-    def send_messages(group):
-        for u, (_, src, rel, _, _) in enumerate(entries(group)):
-            message = jnp.dot(msg_ref[rel], vt_ref[src], preferred_element_type=jnp.float32).astype(jnp.bfloat16)
+    def messages_of(picks):
+        return [jnp.dot(msg_ref[rel], kv_ref[1, src], preferred_element_type=jnp.float32) for _, src, rel, _, _ in picks]
+
+    def keep_messages(messages, left):
+        for u, message in enumerate(messages):
             for k in range(heads):
-                lo = u * span + k * block
-                left[k * size : (k + 1) * size, lo : lo + block] = message[k * size : (k + 1) * size]
-
-    def score(group):
+                lo = u * block
+                left[k, :size, lo : lo + block] = message[k * size : (k + 1) * size].astype(jnp.bfloat16)
+
+    def scores_of(picks, right):
+        return [
+            jnp.dot(kv_ref[0, src], right[u], preferred_element_type=jnp.float32)
+            for u, (_, src, _, _, _) in enumerate(picks)
+        ]
+
+    def keep_scores(picks, found, scores, peak):
         best = [None] * heads
-        for u, (slot, src, _, _, valid) in enumerate(entries(group)):
-            found = jnp.dot(k_ref[src], right[u], preferred_element_type=jnp.float32)
+        for u, (slot, _, _, _, valid) in enumerate(picks):
             tile_words = bits_ref[slot] & valid
             edges = jnp.concatenate([(tile_words[w : w + 1] & bit_of) != 0 for w in range(words)], axis=0)
             for k in range(heads):
-                masked = jnp.where(edges, found[:, k * block : (k + 1) * block], NEG)
+                masked = jnp.where(edges, found[u][:, k * block : (k + 1) * block], NEG)
                 scores[u * heads + k] = masked
                 top = jnp.max(masked.reshape(block // 8, 8, block), axis=0)
                 best[k] = top if best[k] is None else jnp.maximum(best[k], top)
         for k in range(heads):
             peak[k : k + 1] = jnp.max(best[k], axis=0, keepdims=True)
 
-    def gather(group):
-        dst = entries(group)[0][3]
-        keeps, weights = [], [None] * (GROUP * heads)
+    def gather(dst, left, scores, peak):
+        outs = []
         for k in range(heads):
             old = top_ref[dst, k : k + 1]
             new = jnp.maximum(old, peak[k : k + 1])
             top_ref[dst, k : k + 1] = new
-            keeps.append(jnp.exp(old - new))
-            for u in range(GROUP):
-                weights[u * heads + k] = jnp.exp(scores[u * heads + k] - new).astype(jnp.bfloat16)
-        out = jnp.dot(left[...], jnp.concatenate(weights, axis=0), preferred_element_type=jnp.float32)
-        for k in range(heads):
-            rows = slice(k * size, (k + 1) * size)
-            acc_ref[dst, rows] = acc_ref[dst, rows] * keeps[k] + out[rows]
-        keep = jnp.broadcast_to(keeps[0], sum_row.shape)
-        for k in range(1, heads):
-            keep = jnp.where(sum_row == k, keeps[k], keep)
-        acc_ref[dst, cols:] = acc_ref[dst, cols:] * keep + out[cols:]
-
-    def visit(group, carry):
-        gather(group)
-        score(group + 1)
-        send_messages(group + 1)
-        turn(group + 2)
+            weights = [jnp.exp(scores[u * heads + k] - new).astype(jnp.bfloat16) for u in range(GROUP)]
+            out = jnp.dot(left[k], jnp.concatenate(weights, axis=0), preferred_element_type=jnp.float32)
+            outs.append((jnp.exp(old - new), out))
+        for k, (keep, out) in enumerate(outs):
+            acc_ref[dst, k] = acc_ref[dst, k] * keep + out
+
+    def visit(pair, carry):
+        picks = [entries(pair * 2 + i) for i in range(4)]
+        for i in range(2):
+            now, soon, later = picks[i : i + 3]
+            this, other = i, 1 - i
+            keep_messages(messages_of(soon), lefts[other])
+            found = scores_of(soon, rights[other])
+            keep_turned(later, turned_of(later), rights[this])
+            gather(now[0][3], lefts[this], scoress[this], peaks[this])
+            keep_scores(soon, found, scoress[other], peaks[other])
         return carry
 
-    turn(0)
-    score(0)
-    send_messages(0)
-    turn(1)
-    lax.fori_loop(0, groups, visit, 0)
-
-
-def finish_kernel(n_rel, n_head, heads, acc_ref, types_ref, skip_ref, feat_ref, w_ref, *refs):
-    out_ref, hid_out, hid_got, resid, send_sem, recv_sem, local = refs
-    own_blocks, _, block = acc_ref.shape
+    first = entries(0)
+    keep_turned(first, turned_of(first), rights[0])
+    keep_scores(first, scores_of(first, rights[0]), scoress[0], peaks[0])
+    keep_messages(messages_of(first), lefts[0])
+    first = entries(1)
+    keep_turned(first, turned_of(first), rights[1])
+    lax.fori_loop(0, lax.shift_right_logical(groups + 1, 1), visit, 0)
+
+
+def finish_kernel(n_rel, n_head, heads, acc_ref, types_ref, skip_ref, feat_ref, *refs):
+    outs_w, refs = refs[: n_head // 2], refs[n_head // 2 :]
+    out_ref, hid_out, hid_got, resid, w_ref, send_sem, recv_sem, w_send, w_recv, local = refs
+    own_blocks, _, _, block = acc_ref.shape
     kinds = w_ref.shape[1]
     cols = w_ref.shape[2]
     width = w_ref.shape[3]
@@ -420,6 +434,11 @@
 
     fetch = pltpu.make_async_copy(feat_ref.at[pl.ds(pl.multiple_of(h * span, span), span)], resid, local.at[0])
     fetch.start()
+    loads = []
+    for i, got in enumerate(outs_w):
+        head = lax.rem(h + n_head - 2 * i, n_head)
+        loads.append((head, pltpu.make_async_copy(got, w_ref.at[head], local.at[1 + i])))
+        loads[-1][1].start()
     barrier = pltpu.get_barrier_semaphore()
     shifts = [(a, b) for b in range(n_head) for a in range(n_rel) if a or b]
     for a, b in shifts:
@@ -427,10 +446,10 @@
         pl.semaphore_signal(barrier, inc=1, device_id=target)
 
     def hidden_of(source):
-        total = jnp.maximum(acc_ref[source, cols : cols + 8], 1.0)
         sides = []
         for k in range(heads):
-            sides.append(acc_ref[source, pl.ds(k * size, size)] / total[k : k + 1])
+            total = jnp.maximum(acc_ref[source, k, size : size + 1], 1.0)
+            sides.append(acc_ref[source, k, :size] / total)
         agg = jnp.concatenate(sides, axis=0)
         inner = math.sqrt(2.0 / math.pi) * (agg + 0.044715 * (agg * agg * agg))
         hidden = agg * (0.5 * (1.0 + jnp.tanh(inner)))
@@ -455,8 +474,21 @@
         copy.start()
         sends[a, b] = copy
     hid_got[0, 0] = hid_out[0]
+    shared = []
+    for i, (head, load) in enumerate(loads):
+        load.wait()
+        copy = pltpu.make_async_remote_copy(
+            src_ref=w_ref.at[head],
+            dst_ref=w_ref.at[head],
+            send_sem=w_send.at[i],
+            recv_sem=w_recv.at[i],
+            device_id={"head": h + 1 - 2 * lax.rem(h, 2)},
+        )
+        copy.start()
+        shared.append(copy)
     fetch.wait()
-    gates = []
+    for copy in shared:
+        copy.wait_recv()
     for a in range(n_rel):
         source = lax.rem(r + n_rel - a, n_rel)
         for b in range(n_head):
@@ -483,7 +515,7 @@
                     total = jnp.where(masks[kind], outs[kind][i * block : (i + 1) * block, lanes], total)
                 old = resid[rows, lanes].astype(jnp.float32)
                 out_ref[rows, lanes] = (gate * total + (1.0 - gate) * old).astype(jnp.bfloat16)
-    for copy in sends.values():
+    for copy in list(sends.values()) + shared:
         copy.wait_send()
 
 
@@ -530,7 +562,7 @@
 
     bits = tile_bits.transpose(0, 1, 3, 2).reshape(slots, words, block)
 
-    list_rows = -(-(all_slots + own_blocks * GROUP + 3 * GROUP) // block) + 1
+    list_rows = -(-(all_slots + own_blocks * GROUP + 4 * GROUP) // block) + 1
     chunks = blocks // CHUNK
     half = max(n_head // 2 - 1, 1)
     dma = pltpu.SemaphoreType.DMA
@@ -548,23 +580,18 @@
         w_key,
         w_value,
         w_query,
-        rel_att,
         rel_msg,
-        w_out,
         bits,
     )
-    keys, values_t, query_t, att, msg, all_bits, all_out, listed = pl.pallas_call(
+    pairs_kv, query_t, msg, all_bits, listed = pl.pallas_call(
         functools.partial(prepare_kernel, n_rel, n_node, n_head, fields),
-        in_specs=[hbm] * 13,
-        out_specs=[vmem] * 8,
+        in_specs=[hbm] * 11,
+        out_specs=[vmem] * 5,
         out_shape=[
-            shape((n_node * blocks, block, cols), bf),
-            shape((n_node * blocks, cols, block), bf),
+            shape((2, n_node * blocks, block, cols), bf),
             shape((own_blocks, cols, block), bf),
             shape((relations, cols, cols), bf),
-            shape((relations, cols, cols), bf),
             shape((all_slots, words, block), jnp.int32),
-            shape((n_head,) + w_out.shape, bf),
             shape((list_rows, block), jnp.int32),
         ],
         scratch_shapes=[
@@ -572,7 +599,6 @@
             pltpu.VMEM(w_key.shape, bf),
             pltpu.VMEM(w_value.shape, bf),
             pltpu.VMEM(w_query.shape, bf),
-            pltpu.VMEM(rel_att.shape, bf),
             pltpu.VMEM(rel_msg.shape, bf),
             pltpu.VMEM((n_rel, 8, block), jnp.int32),
             pltpu.VMEM((blocks, block), jnp.int32),
@@ -591,47 +617,54 @@
             dma((n_rel,)),
             dma((n_node, chunks, 2)),
             dma((n_node, chunks, 2)),
-            dma((n_head,)),
-            dma((n_head,)),
+            dma((n_node, chunks)),
+            dma((n_node, chunks)),
         ],
         compiler_params=pltpu.CompilerParams(collective_id=0, has_side_effects=True, vmem_limit_bytes=VMEM_BYTES),
         name="prepare",
     )(*[in_hbm(value) for value in operands])
 
-    tall = cols + PAD_ROWS
+    tall = cols // heads + PAD_ROWS
     acc = pl.pallas_call(
         functools.partial(tile_kernel, heads, factor, fields),
-        in_specs=[smem] * 2 + [vmem] * 6,
+        in_specs=[smem] * 2 + [vmem] * 5,
         out_specs=vmem,
-        out_shape=shape((own_blocks, tall, block), jnp.float32),
+        out_shape=shape((own_blocks, heads, tall, block), jnp.float32),
         scratch_shapes=[
             pltpu.VMEM((own_blocks, 8, block), jnp.float32),
-            pltpu.VMEM((tall, GROUP * heads * block), bf),
-            pltpu.VMEM((GROUP, cols, heads * block), bf),
-            pltpu.VMEM((GROUP * heads, block, block), jnp.float32),
-            pltpu.VMEM((8, block), jnp.float32),
+            *[pltpu.VMEM((heads, tall, GROUP * block), bf)] * 2,
+            *[pltpu.VMEM((GROUP, cols, heads * block), bf)] * 2,
+            *[pltpu.VMEM((GROUP * heads, block, block), jnp.float32)] * 2,
+            *[pltpu.VMEM((8, block), jnp.float32)] * 2,
         ],
         compiler_params=pltpu.CompilerParams(vmem_limit_bytes=VMEM_BYTES),
         name="tiles",
-    )(listed, rel_prior.T, query_t, keys, values_t, all_bits, att, msg)
-
+    )(listed, rel_prior.T, query_t, pairs_kv, all_bits, rel_att, msg)
+
+    gathered = [w_out]
+    for shift in range(2, n_head, 2):
+        pairs = [(i, (i + shift) % n_head) for i in range(n_head)]
+        gathered.append(lax.ppermute(w_out, "head", pairs))
     piece = own_blocks // n_head * block
     return pl.pallas_call(
         functools.partial(finish_kernel, n_rel, n_head, heads),
-        in_specs=[vmem, vmem, smem, hbm, vmem],
+        in_specs=[vmem, vmem, smem, hbm, hbm] + [vmem] * (len(gathered) - 1),
         out_specs=vmem,
         out_shape=shape((n_rel * piece, width), bf),
         scratch_shapes=[
             pltpu.VMEM((n_head, piece, cols), bf),
             pltpu.VMEM((n_rel, n_head, piece, cols), bf),
             pltpu.VMEM((n_rel * piece, width), bf),
+            pltpu.VMEM((n_head,) + w_out.shape, bf),
             dma((n_rel, n_head)),
             dma((n_rel, n_head)),
-            dma((1,)),
+            dma((n_head,)),
+            dma((n_head,)),
+            dma((1 + n_head,)),
         ],
         compiler_params=pltpu.CompilerParams(collective_id=1, has_side_effects=True, vmem_limit_bytes=VMEM_BYTES),
         name="finish",
-    )(acc, node_type.reshape(blocks, block), skip, in_hbm(features), all_out)
+    )(acc, node_type.reshape(blocks, block), skip, in_hbm(features), in_hbm(w_out), *gathered[1:])
 
 
 def solution(mesh):

time: 66.1 us -> 57.3 us (0.87)
  Pallas kernels: 64.8 us -> 54.4 us
  starting transfers between devices: 0 us -> 2.06 us
    pallas_call x1, Pallas kernels: 33.1 us -> 23.3 us  [per_device(): pl.pallas_call(functools.partial(prepare_kernel, n_rel, n_node, n_head, f...]
    pallas_call x1, Pallas kernels: 14.8 us -> 9.64 us  [per_device(): pl.pallas_call(functools.partial(tile_kernel, heads, factor, fields), in_...]
    pallas_call x1, Pallas kernels: 17 us -> 21.4 us  [per_device(): pl.pallas_call(functools.partial(finish_kernel, n_rel, n_head, heads), in...]
    ppermute x0 -> x1, starting transfers between devices: none -> 2.06 us  [per_device(): gathered.append(lax.ppermute(w_out, 'head', pairs))]
  transfers between devices with their start and end apart: 0 -> 1, of which waited for: 0 -> 0; matrix products, arithmetic and copies ran while one was open for 0% -> 0% of each run, Pallas kernels for 0% -> 58%
where the time goes in v2:
time: 57.3 us
  Pallas kernels  54.4 us (95%)
  starting transfers between devices  2.06 us (4%)
  local copies, waits for them, and re-layouts  0.82 us (1%)
    pallas_call x1, Pallas kernels, per_device(): pl.pallas_call(functools.partial(prepare_kernel, n_rel, n_node, n_head, f...  23.3 us
    pallas_call x1, Pallas kernels, per_device(): pl.pallas_call(functools.partial(finish_kernel, n_rel, n_head, heads), in...  21.4 us
    pallas_call x1, Pallas kernels, per_device(): pl.pallas_call(functools.partial(tile_kernel, heads, factor, fields), in_...  9.64 us
    ppermute x1, starting transfers between devices, per_device(): gathered.append(lax.ppermute(w_out, 'head', pairs))  2.06 us
  transfers between devices with their start and end apart: 1, of which 0 were waited for; matrix products, arithmetic and copies ran while one was open for 0% of the time, Pallas kernels for 58%

profile of v2, /device:TPU:1, one launch (start us, length us, event | category | flops | bytes accessed | tf_op | source)
XLA Modules:
  0.0 57.3 jit_solution(13172111086169836976)
XLA Ops:
  0.0 2.1 %collective-permute-start = (bf16[4,128,512]{2,1,0:T(8,128)(2,1)}, bf16[4,128,512]{2,1,0:T(8,128)(2,1)S(1)}, u32[]{:S(2)}, u32[]{:S(2)}) collective-permute-start(bf16[4,128,512]{2,1,0:T(8,128)(2,1)} %refs_0_.1), channel_id=1, source_target_pairs={{0,2},{1,3},{2,0},{3,1},{4,6},{5,7},{6,4},{7,5},{8,10},{9,11},{10,... | collective-permute-start | bytes 1572872 | tf_op jit(solution)/shard_map/ppermute | solution.py:647
  2.1 0.0 copy-start
  2.1 0.0 copy-start.2
  2.1 23.3 %prepare.1 = (bf16[2,32,128,128]{3,2,1,0:T(8,128)(2,1)S(1)}, bf16[4,128,128]{2,1,0:T(8,128)(2,1)S(1)}, bf16[64,128,128]{2,1,0:T(8,128)(2,1)S(1)}, s32[1024,4,128]{2,1,0:T(4,128)S(1)}, s32[10,128]{1,0:T(8,128)S(1)}) custom-call(s32[16,128]{1,0:T(8,128)} %bitcast.7, s32[16,16]{1,0:T(8,128)} %refs_1_.1, s32[16,16]{1,0:T(8,128)} %refs_2_.1, s32[1,16]{1,0:T(1,128)} %bitcast.11, ...), custom_call_target="tpu_custom_call" | custom-call | tf_op jit(solution)/shard_map/prepare/pallas_call | solution.py:586
  25.4 0.0 copy-done
  25.4 0.0 copy-done.2
  25.4 0.0 copy-start.1
  25.4 0.0 copy-start.3
  25.4 9.6 %tiles.1.acc_ref = f32[4,2,80,128]{3,2,1,0:T(8,128)S(1)} custom-call(s32[10,128]{1,0:T(8,128)S(1)} %get-tuple-element.10.list_ref, f32[2,64]{1,0:T(2,128)S(1)} %bitcast.9, bf16[4,128,128]{2,1,0:T(8,128)(2,1)S(1)} %get-tuple-element.11.qt_ref, bf16[2,32,128,128]{3,2,1,0:T(8,128)(2,1)S(1)} %get-tuple-element.12.kv_ref, ...), custom_call_target="tpu_custom_call" | custom-call | tf_op jit(solution)/shard_map/tiles/pallas_call | solution.py:628
  35.1 0.0 collective-permute-done.refs_1_
  35.1 0.0 copy-done.1
  35.1 0.0 copy-done.3
  35.1 21.4 %finish.1 = bf16[512,512]{1,0:T(8,128)(2,1)S(1)} custom-call(f32[4,2,80,128]{3,2,1,0:T(8,128)S(1)} %tiles.1.acc_ref, s32[16,128]{1,0:T(8,128)S(1)} %bitcast.8, f32[4]{0:T(128)S(1)} %copy-done.3, bf16[2048,512]{1,0:T(8,128)(2,1)} %feat_ref.1, bf16[4,128,512]{2,1,0:T(8,128)(2,1)} %refs_0_.1, bf16[4,128,512]{2,1,0:T(8,128)(2,1)S(1)} %collective-permute-done.refs_1_), custom_call_target="tpu_custom_call" | custom-call | tf_op jit(solution)/shard_map/finish/pallas_call | solution.py:649
  56.5 0.8 %copy.17 = bf16[512,512]{1,0:T(8,128)(2,1)} copy(bf16[512,512]{1,0:T(8,128)(2,1)S(1)} %finish.1) | data formatting | bytes 1048576
Async XLA Ops:
  0.0 35.1 %collective-permute-start = (bf16[4,128,512]{2,1,0:T(8,128)(2,1)}, bf16[4,128,512]{2,1,0:T(8,128)(2,1)S(1)}, u32[]{:S(2)}, u32[]{:S(2)}) collective-permute-start(bf16[4,128,512]{2,1,0:T(8,128)(2,1)} %refs_0_.1), channel_id=1, source_target_pairs={{0,2},{1,3},{2,0},{3,1},{4,6},{5,7},{6,4},{7,5},{8,10},{9,11},{10,... | collective-permute-start | bytes 1572872 | tf_op jit(solution)/shard_map/ppermute | solution.py:647
  2.1 23.3 %copy-start = (bf16[64,2,64,64]{3,2,1,0:T(8,128)(2,1)S(1)}, bf16[64,2,64,64]{3,2,1,0:T(8,128)(2,1)}, u32[]{:S(2)}) copy-start(bf16[64,2,64,64]{3,2,1,0:T(8,128)(2,1)} %att_ref.1) | copy-start | bytes 3145732
  2.1 23.4 %copy-start.2 = (f32[64,2]{0,1:T(2,128)S(1)}, f32[64,2]{0,1:T(2,128)}, u32[]{:S(2)}) copy-start(f32[64,2]{0,1:T(2,128)} %param.22) | copy-start | bytes 1540
  25.4 9.7 %copy-start.1 = (s32[2048]{0:T(1024)S(1)}, s32[2048]{0:T(1024)}, u32[]{:S(2)}) copy-start(s32[2048]{0:T(1024)} %param.16) | copy-start | bytes 24580
  25.4 9.7 %copy-start.3 = (f32[4]{0:T(128)S(1)}, f32[4]{0:T(128)}, u32[]{:S(2)}) copy-start(f32[4]{0:T(128)} %skip_ref.1) | copy-start | bytes 52

commit v3 on v2

--- a/solution.py
+++ b/solution.py
@@ -14,6 +14,7 @@
 CHUNK = 4
 SPLIT = 3
 BATCH = 8
+PIECES = 2
 PAD_ROWS = 16
 VMEM_BYTES = 30 * 1024 * 1024
 
@@ -35,8 +36,18 @@
     return (local // per) * per * n_rel + r * per + local % per
 
 
-def project_rows(x, weights):
-    return [jnp.dot(x, w, preferred_element_type=jnp.float32) for w in weights]
+def along_rel(n_rel, r):
+    if n_rel == 4:
+        peers = {2: lax.rem(r + 2, 4), 1: r + 1 - 2 * lax.rem(r, 2), 3: 3 - r}
+        return {u: (peer, peer) for u, peer in peers.items()}, (r == 1) | (r == 2)
+    return {u: (lax.rem(r + u, n_rel), lax.rem(r + n_rel - u, n_rel)) for u in range(1, n_rel)}, None
+
+
+def only_if(condition, action):
+    if condition is None:
+        action()
+    else:
+        pl.when(condition)(action)
 
 
 def compact(meta, own_blocks, per, n_rel, r, fields, list_ref):
@@ -126,7 +137,7 @@
     (kv_all, qt_ref, msg_out, bits_all, list_ref) = refs[:5]
     (x_v, wk_v, wv_v, wq_v, msg_v, meta_all), refs = refs[5:11], refs[11:]
     (types_ref, src_v, dst_v, count_v, perm_v), refs = refs[:5], refs[5:]
-    (local, z_send, z_recv, y_send, y_recv, d_send, d_recv, m_send, m_recv, x_send, x_recv, f_send, f_recv) = refs
+    (local, z_send, z_recv, v_send, y_send, y_recv, d_send, d_recv, m_send, m_recv, x_send, x_recv, f_send, f_recv) = refs
     blocks = types_ref.shape[0]
     block = types_ref.shape[1]
     cols = wk_v.shape[2]
@@ -175,7 +186,7 @@
     meta_all[pl.ds(r, 1)] = pack(src_v[...], dst_v[...], count_v[...], perm_v[...], fields, block)
     pl.semaphore_wait(barrier, n_rel - 1 + n_node - 1 + len(pairs) + 1)
 
-    started = []
+    started, guarded = [], []
 
     def send(src, dst, send_sem, recv_sem, target):
         copy = pltpu.make_async_remote_copy(
@@ -185,17 +196,35 @@
         started.append(copy)
         return copy
 
-    def bit_rows(rel, head):
-        return bits_all.at[pl.ds(pl.multiple_of(rel * slots + head * share, share), share)]
+    steps, inner = along_rel(n_rel, r)
+    relayed = 3 if inner is not None else None
+    part_rows = share // PIECES
+
+    def bit_rows(rel, head, piece):
+        first = rel * slots + head * share + piece * part_rows
+        return bits_all.at[pl.ds(pl.multiple_of(first, part_rows), part_rows)]
+
+    def send_bits(rel, head, piece, sems, index, target, condition=None):
+        rows = bit_rows(rel, head, piece)
+        copy = pltpu.make_async_remote_copy(
+            src_ref=rows,
+            dst_ref=rows,
+            send_sem=sems[0].at[index],
+            recv_sem=sems[1].at[index],
+            device_id=target,
+        )
+        only_if(condition, copy.start)
+        guarded.append((condition, copy))
+        return copy
 
     own_bits.wait()
-    metas, zs = [], []
-    for t in range(1, n_rel):
-        target = {"rel": lax.rem(r + t, n_rel)}
-        metas.append(send(meta_all.at[r], meta_all.at[r], m_send.at[t], m_recv.at[t], target))
-    for t in range(1, n_rel):
-        target = {"rel": lax.rem(r + t, n_rel)}
-        zs.append(send(bit_rows(r, h), bit_rows(r, h), z_send.at[t], z_recv.at[t], target))
+    metas, zs = [], {}
+    for u, (peer, _) in steps.items():
+        metas.append(send(meta_all.at[r], meta_all.at[r], m_send.at[u], m_recv.at[u], {"rel": peer}))
+    for u, (peer, _) in steps.items():
+        for q in range(PIECES):
+            condition = inner if u == relayed else None
+            zs[u, q] = send_bits(r, h, q, (z_send, z_recv), (u, q), {"rel": peer}, condition)
 
     for copy in got_w:
         copy.wait()
@@ -267,41 +296,39 @@
         return carry
 
     ys, ds = [], []
-    for t in range(1, n_rel):
-        zs[t - 1].wait_recv()
-        source = lax.rem(r + n_rel - t, n_rel)
-        for i, u in enumerate(pairs):
-            target = {"head": lax.rem(h + u, n_head)}
-            ys.append((t, u, send(bit_rows(source, h), bit_rows(source, h), y_send.at[t, i], y_recv.at[t, i], target)))
-        ds.append(
-            send(bit_rows(source, h), bit_rows(source, h), d_send.at[t, 0], d_recv.at[t, 0], {"head": sibling})
-        )
-        if t == 1:
-            lax.fori_loop(0, relations // BATCH, relation, 0)
-            for copy in metas:
-                copy.wait_recv()
-            used = slots // block
-            meta = jnp.concatenate([meta_all[s, :used] for s in range(n_rel)], axis=0)
-            compact(meta, own_blocks, per, n_rel, r, fields, list_ref)
-        if t - 1 < SPLIT:
-            forward(t - 1)
+    for turn, (u, (_, source)) in enumerate(steps.items()):
+        for q in range(PIECES):
+            zs[u, q].wait_recv()
+            if relayed and u == 2:
+                send_bits(source, h, q, (v_send, z_recv), (relayed, q), {"rel": steps[1][0]}, inner)
+            for i, t in enumerate(pairs):
+                target = {"head": lax.rem(h + t, n_head)}
+                ys.append((source, u, q, t, send_bits(source, h, q, (y_send, y_recv), (u, q, i), target)))
+            ds.append(send_bits(source, h, q, (d_send, d_recv), (u, q, 0), {"head": sibling}))
+        if turn < SPLIT:
+            forward(turn)
+
+    lax.fori_loop(0, relations // BATCH, relation, 0)
+    for copy in metas:
+        copy.wait_recv()
+    used = slots // block
+    meta = jnp.concatenate([meta_all[s, :used] for s in range(n_rel)], axis=0)
+    compact(meta, own_blocks, per, n_rel, r, fields, list_ref)
 
     for c in range(n_rel - 1, SPLIT):
         forward(c)
-    for t, u, copy in ys:
+    for source, u, q, t, copy in ys:
         copy.wait_recv()
-        source = lax.rem(r + n_rel - t, n_rel)
-        head = lax.rem(h + n_head - u, n_head)
-        which = 1 + pairs.index(u)
-        ds.append(
-            send(bit_rows(source, head), bit_rows(source, head), d_send.at[t, which], d_recv.at[t, which], {"head": sibling})
-        )
+        head = lax.rem(h + n_head - t, n_head)
+        ds.append(send_bits(source, head, q, (d_send, d_recv), (u, q, 1 + pairs.index(t)), {"head": sibling}))
     for copy in ds:
         copy.wait_recv()
     for copy in xs:
         copy.wait_recv()
     for copy in started:
         copy.wait_send()
+    for condition, copy in guarded:
+        only_if(condition, copy.wait_send)
 
 
 def tile_kernel(heads, factor, fields, list_ref, prior_ref, qt_ref, kv_ref, bits_ref, att_ref, msg_ref, *refs):
@@ -420,7 +447,7 @@
 
 def finish_kernel(n_rel, n_head, heads, acc_ref, types_ref, skip_ref, feat_ref, *refs):
     outs_w, refs = refs[: n_head // 2], refs[n_head // 2 :]
-    out_ref, hid_out, hid_got, resid, w_ref, send_sem, recv_sem, w_send, w_recv, local = refs
+    out_ref, hid_out, hid_got, resid, w_ref, send_sem, recv_sem, relay_sem, w_send, w_recv, local = refs
     own_blocks, _, _, block = acc_ref.shape
     kinds = w_ref.shape[1]
     cols = w_ref.shape[2]
@@ -439,11 +466,13 @@
         head = lax.rem(h + n_head - 2 * i, n_head)
         loads.append((head, pltpu.make_async_copy(got, w_ref.at[head], local.at[1 + i])))
         loads[-1][1].start()
+    steps, inner = along_rel(n_rel, r)
+    relayed = 3 if inner is not None else None
+    steps[0] = (r, r)
     barrier = pltpu.get_barrier_semaphore()
-    shifts = [(a, b) for b in range(n_head) for a in range(n_rel) if a or b]
-    for a, b in shifts:
-        target = {"rel": lax.rem(r + a, n_rel), "head": lax.rem(h + b, n_head)}
-        pl.semaphore_signal(barrier, inc=1, device_id=target)
+    shifts = [(u, b) for u in steps for b in range(n_head) if u or b]
+    for u, b in shifts:
+        pl.semaphore_signal(barrier, inc=1, device_id={"rel": steps[u][0], "head": lax.rem(h + b, n_head)})
 
     def hidden_of(source):
         sides = []
@@ -461,18 +490,23 @@
             hid_out[b, i * block : (i + 1) * block] = hidden_of(head * per + i)
     pl.semaphore_wait(barrier, len(shifts))
 
-    sends = {}
-    for a, b in sorted(shifts, key=lambda s: (s[0] == 0, s[1])):
-        target = {"rel": lax.rem(r + a, n_rel), "head": lax.rem(h + b, n_head)}
+    sends, guarded = {}, []
+
+    def pass_on(source, u, b, sem, target, condition):
         copy = pltpu.make_async_remote_copy(
-            src_ref=hid_out.at[b],
-            dst_ref=hid_got.at[a, b],
-            send_sem=send_sem.at[a, b],
-            recv_sem=recv_sem.at[a, b],
+            src_ref=source,
+            dst_ref=hid_got.at[u, b],
+            send_sem=sem.at[u, b],
+            recv_sem=recv_sem.at[u, b],
             device_id=target,
         )
-        copy.start()
-        sends[a, b] = copy
+        only_if(condition, copy.start)
+        guarded.append((condition, copy))
+        return copy
+
+    for u, b in shifts:
+        target = {"rel": steps[u][0], "head": lax.rem(h + b, n_head)}
+        sends[u, b] = pass_on(hid_out.at[b], u, b, send_sem, target, inner if u == relayed else None)
     hid_got[0, 0] = hid_out[0]
     shared = []
     for i, (head, load) in enumerate(loads):
@@ -489,12 +523,15 @@
     fetch.wait()
     for copy in shared:
         copy.wait_recv()
-    for a in range(n_rel):
-        source = lax.rem(r + n_rel - a, n_rel)
+    order = [u for u in (2, 0, 1, 3) if u in steps] + [u for u in steps if u > 3]
+    for u in order:
+        source = steps[u][1]
         for b in range(n_head):
-            if a or b:
-                sends[a, b].wait_recv()
-        parts = [hid_got[a, lax.rem(h + n_head - head, n_head)] for head in range(n_head)]
+            if u or b:
+                sends[u, b].wait_recv()
+                if relayed and u == 2:
+                    pass_on(hid_got.at[u, b], relayed, b, relay_sem, {"rel": steps[1][0]}, inner)
+        parts = [hid_got[u, lax.rem(h + n_head - head, n_head)] for head in range(n_head)]
         hidden = jnp.concatenate(parts, axis=1)
         outs = []
         for kind in range(kinds):
@@ -515,8 +552,10 @@
                     total = jnp.where(masks[kind], outs[kind][i * block : (i + 1) * block, lanes], total)
                 old = resid[rows, lanes].astype(jnp.float32)
                 out_ref[rows, lanes] = (gate * total + (1.0 - gate) * old).astype(jnp.bfloat16)
-    for copy in list(sends.values()) + shared:
+    for copy in shared:
         copy.wait_send()
+    for condition, copy in guarded:
+        only_if(condition, copy.wait_send)
 
 
 def per_device(
@@ -607,12 +646,13 @@
             pltpu.VMEM((1, positions), jnp.int32),
             pltpu.VMEM((1, positions), jnp.int32),
             dma((13 + chunks,)),
-            dma((n_rel,)),
-            dma((n_rel,)),
-            dma((n_rel, half)),
-            dma((n_rel, half)),
-            dma((n_rel, 1 + half)),
-            dma((n_rel, 1 + half)),
+            dma((n_rel, PIECES)),
+            dma((n_rel, PIECES)),
+            dma((n_rel, PIECES)),
+            dma((n_rel, PIECES, half)),
+            dma((n_rel, PIECES, half)),
+            dma((n_rel, PIECES, 1 + half)),
+            dma((n_rel, PIECES, 1 + half)),
             dma((n_rel,)),
             dma((n_rel,)),
             dma((n_node, chunks, 2)),
@@ -624,6 +664,11 @@
         name="prepare",
     )(*[in_hbm(value) for value in operands])
 
+    late_out, listed = lax.optimization_barrier((w_out, listed))
+    gathered = [w_out]
+    for shift in range(2, n_head, 2):
+        pairs = [(i, (i + shift) % n_head) for i in range(n_head)]
+        gathered.append(lax.ppermute(late_out, "head", pairs))
     tall = cols // heads + PAD_ROWS
     acc = pl.pallas_call(
         functools.partial(tile_kernel, heads, factor, fields),
@@ -641,10 +686,6 @@
         name="tiles",
     )(listed, rel_prior.T, query_t, pairs_kv, all_bits, rel_att, msg)
 
-    gathered = [w_out]
-    for shift in range(2, n_head, 2):
-        pairs = [(i, (i + shift) % n_head) for i in range(n_head)]
-        gathered.append(lax.ppermute(w_out, "head", pairs))
     piece = own_blocks // n_head * block
     return pl.pallas_call(
         functools.partial(finish_kernel, n_rel, n_head, heads),
@@ -656,6 +697,7 @@
             pltpu.VMEM((n_rel, n_head, piece, cols), bf),
             pltpu.VMEM((n_rel * piece, width), bf),
             pltpu.VMEM((n_head,) + w_out.shape, bf),
+            dma((n_rel, n_head)),
             dma((n_rel, n_head)),
             dma((n_rel, n_head)),
             dma((n_head,)),

time: 57.3 us -> 53.6 us (0.935); the launches traced: 57.3 us -> 52.7 us
  Pallas kernels: 54.4 us -> 49.6 us
  waiting for transfers between devices: 0.01 us -> 0.89 us
  starting transfers between devices: 2.06 us -> 1.34 us
    pallas_call x1, Pallas kernels: 21.4 us -> 15.7 us  [per_device(): pl.pallas_call(functools.partial(finish_kernel, n_rel, n_head, heads), in...]
    ppermute x1, waiting for transfers between devices: 0.01 us -> 0.89 us  [per_device(): gathered.append(lax.ppermute(late_out, 'head', pairs))]
    ppermute x1, starting transfers between devices: 2.06 us -> 1.34 us  [per_device(): gathered.append(lax.ppermute(late_out, 'head', pairs))]
    pallas_call x1, Pallas kernels: 9.64 us -> 10.3 us  [per_device(): pl.pallas_call(functools.partial(tile_kernel, heads, factor, fields), in_...]
  transfers between devices with their start and end apart: 1 -> 1, of which waited for: 0 -> 1; matrix products, arithmetic and copies ran while one was open for 0% -> 0% of each run, Pallas kernels for 58% -> 20%
where the time goes in v3:
time: 53.6 us; the launch traced here: 52.7 us
  Pallas kernels  49.6 us (93%)
  starting transfers between devices  1.34 us (2%)
  waiting for transfers between devices  0.89 us (2%)
  local copies, waits for them, and re-layouts  0.81 us (2%)
    pallas_call x1, Pallas kernels, per_device(): pl.pallas_call(functools.partial(prepare_kernel, n_rel, n_node, n_head, f...  23.6 us
    pallas_call x1, Pallas kernels, per_device(): pl.pallas_call(functools.partial(finish_kernel, n_rel, n_head, heads), in...  15.7 us
    pallas_call x1, Pallas kernels, per_device(): pl.pallas_call(functools.partial(tile_kernel, heads, factor, fields), in_...  10.3 us
    ppermute x1, starting transfers between devices, per_device(): gathered.append(lax.ppermute(late_out, 'head', pairs))  1.34 us
  transfers between devices with their start and end apart: 1, of which 1 were waited for; matrix products, arithmetic and copies ran while one was open for 0% of the time, Pallas kernels for 20%

profile of v3, /device:TPU:1, one launch (start us, length us, event | category | flops | bytes accessed | tf_op | source)
XLA Modules:
  0.0 52.7 jit_solution(12851741778106959518)
XLA Ops:
  0.0 0.0 copy-start.4
  0.0 0.0 copy-start
  0.0 0.0 copy-start.2
  0.0 23.6 %prepare.1 = (bf16[2,32,128,128]{3,2,1,0:T(8,128)(2,1)S(1)}, bf16[4,128,128]{2,1,0:T(8,128)(2,1)S(1)}, bf16[64,128,128]{2,1,0:T(8,128)(2,1)S(1)}, s32[1024,4,128]{2,1,0:T(4,128)S(1)}, s32[10,128]{1,0:T(8,128)S(1)}) custom-call(s32[16,128]{1,0:T(8,128)} %bitcast.7, s32[16,16]{1,0:T(8,128)} %refs_1_.1, s32[16,16]{1,0:T(8,128)} %refs_2_.1, s32[1,16]{1,0:T(1,128)} %bitcast.11, ...), custom_call_target="tpu_custom_call" | custom-call | tf_op jit(solution)/shard_map/prepare/pallas_call | solution.py:625
  23.6 0.0 copy-done.4
  23.6 1.3 %collective-permute-start = (bf16[4,128,512]{2,1,0:T(8,128)(2,1)S(1)}, bf16[4,128,512]{2,1,0:T(8,128)(2,1)S(1)}, u32[]{:S(2)}, u32[]{:S(2)}) collective-permute-start(bf16[4,128,512]{2,1,0:T(8,128)(2,1)S(1)} %copy-done.4), channel_id=1, source_target_pairs={{0,2},{1,3},{2,0},{3,1},{4,6},{5,7},{6,4},{7,5},{8,10},{9,11},{10,... | collective-permute-start | bytes 1572872 | tf_op jit(solution)/shard_map/ppermute | solution.py:671
  25.0 0.0 copy-done
  25.0 0.0 copy-done.2
  25.0 0.0 copy-start.1
  25.0 0.0 copy-start.3
  25.0 10.3 %tiles.1.acc_ref = f32[4,2,80,128]{3,2,1,0:T(8,128)S(1)} custom-call(s32[10,128]{1,0:T(8,128)S(1)} %get-tuple-element.13.list_ref, f32[2,64]{1,0:T(2,128)S(1)} %bitcast.9, bf16[4,128,128]{2,1,0:T(8,128)(2,1)S(1)} %get-tuple-element.14.qt_ref, bf16[2,32,128,128]{3,2,1,0:T(8,128)(2,1)S(1)} %get-tuple-element.15.kv_ref, ...), custom_call_target="tpu_custom_call" | custom-call | tf_op jit(solution)/shard_map/tiles/pallas_call | solution.py:673
  35.3 0.9 %collective-permute-done.refs_1_ = bf16[4,128,512]{2,1,0:T(8,128)(2,1)S(1)} collective-permute-done((bf16[4,128,512]{2,1,0:T(8,128)(2,1)S(1)}, bf16[4,128,512]{2,1,0:T(8,128)(2,1)S(1)}, u32[]{:S(2)}, u32[]{:S(2)}) %collective-permute-start) | collective-permute-done | bytes 524320 | tf_op jit(solution)/shard_map/ppermute | solution.py:671
  36.2 0.0 copy-done.1
  36.2 0.0 copy-done.3
  36.2 15.7 %finish.1 = bf16[512,512]{1,0:T(8,128)(2,1)S(1)} custom-call(f32[4,2,80,128]{3,2,1,0:T(8,128)S(1)} %tiles.1.acc_ref, s32[16,128]{1,0:T(8,128)S(1)} %bitcast.8, f32[4]{0:T(128)S(1)} %copy-done.3, bf16[2048,512]{1,0:T(8,128)(2,1)} %feat_ref.1, bf16[4,128,512]{2,1,0:T(8,128)(2,1)} %refs_0_.1, bf16[4,128,512]{2,1,0:T(8,128)(2,1)S(1)} %collective-permute-done.refs_1_), custom_call_target="tpu_custom_call" | custom-call | tf_op jit(solution)/shard_map/finish/pallas_call | solution.py:690
  51.9 0.8 %copy.17 = bf16[512,512]{1,0:T(8,128)(2,1)} copy(bf16[512,512]{1,0:T(8,128)(2,1)S(1)} %finish.1) | data formatting | bytes 1048576
Async XLA Ops:
  0.0 23.6 %copy-start.4 = (bf16[4,128,512]{2,1,0:T(8,128)(2,1)S(1)}, bf16[4,128,512]{2,1,0:T(8,128)(2,1)}, u32[]{:S(2)}) copy-start(bf16[4,128,512]{2,1,0:T(8,128)(2,1)} %refs_0_.1) | copy-start | bytes 1572868
  0.0 25.0 %copy-start = (bf16[64,2,64,64]{3,2,1,0:T(8,128)(2,1)S(1)}, bf16[64,2,64,64]{3,2,1,0:T(8,128)(2,1)}, u32[]{:S(2)}) copy-start(bf16[64,2,64,64]{3,2,1,0:T(8,128)(2,1)} %att_ref.1) | copy-start | bytes 3145732
  0.0 25.0 %copy-start.2 = (f32[64,2]{0,1:T(2,128)S(1)}, f32[64,2]{0,1:T(2,128)}, u32[]{:S(2)}) copy-start(f32[64,2]{0,1:T(2,128)} %param.22) | copy-start | bytes 1540
  23.6 12.6 %collective-permute-start = (bf16[4,128,512]{2,1,0:T(8,128)(2,1)S(1)}, bf16[4,128,512]{2,1,0:T(8,128)(2,1)S(1)}, u32[]{:S(2)}, u32[]{:S(2)}) collective-permute-start(bf16[4,128,512]{2,1,0:T(8,128)(2,1)S(1)} %copy-done.4), channel_id=1, source_target_pairs={{0,2},{1,3},{2,0},{3,1},{4,6},{5,7},{6,4},{7,5},{8,10},{9,11},{10,... | collective-permute-start | bytes 1572872 | tf_op jit(solution)/shard_map/ppermute | solution.py:671
  25.0 11.2 %copy-start.1 = (s32[2048]{0:T(1024)S(1)}, s32[2048]{0:T(1024)}, u32[]{:S(2)}) copy-start(s32[2048]{0:T(1024)} %param.16) | copy-start | bytes 24580
  25.0 11.2 %copy-start.3 = (f32[4]{0:T(128)S(1)}, f32[4]{0:T(128)}, u32[]{:S(2)}) copy-start(f32[4]{0:T(128)} %skip_ref.1) | copy-start | bytes 52
